TPU v7x, 16 devices: a 4x2x1 block of a 4x4x8 slice. The times are simulated.
16 devices in a mesh: batch: 2 (over y, z), dap: 8 (over x, core).
Axes of the slice: x: 4, y: 2, z: 1, core: 2. Of those that a mesh axis runs over, the one named last changes fastest.
The devices are a block of a 4x4x8 slice.
Arguments:
- pair_act: bfloat16 [768, 384, 128], P(('batch', 'dap')), parts along dimension 0
- pair_mask: int32 [768, 384], P(('batch', 'dap')), parts along dimension 0
- ln_in_scale: bfloat16 [2, 128], replicated
- ln_in_bias: bfloat16 [2, 128], replicated
- w_in: bfloat16 [2, 128, 512], replicated
- b_in: bfloat16 [2, 512], replicated
- w_gate: bfloat16 [2, 128, 128], replicated
- b_gate: bfloat16 [2, 128], replicated
- ln_out_scale: bfloat16 [2, 128], replicated
- ln_out_bias: bfloat16 [2, 128], replicated
- w_out: bfloat16 [2, 128, 128], replicated
- b_out: bfloat16 [2, 128], replicated
Outputs:
- output: bfloat16 [768, 384, 128], P(('batch', 'dap')), parts along dimension 0
There are 2 independent parts. A program takes and returns all parts, laid end to end along the dimension named above; an argument that names none is the same for every part.
All inputs are finite; a program needn't handle non-finite values.
Results may differ from a plain program's by a relative error of at most 0.00746292.
Values are sent between devices in bfloat16 or wider.
A program may use at most 768 MiB of HBM per device.

v0:
```python
import functools

import jax
import jax.numpy as jnp
from jax import lax
from jax.experimental import pallas as pl
from jax.experimental.pallas import tpu as pltpu
from jax.sharding import PartitionSpec as P


LN_EPS = 1e-5
F32 = jnp.float32
BF = jnp.bfloat16
RB = 16
LANES = 128
VMEM = 67043328
ROWS_AT_ONCE = 8
ANY = pl.BlockSpec(memory_space=pl.ANY)


def norm_columns(x, scale, bias):
    inv = 1.0 / x.shape[0]
    cen = x - jnp.sum(x, axis=0, keepdims=True) * inv
    var = jnp.sum(cen * cen, axis=0, keepdims=True) * inv
    return (cen * lax.rsqrt(var + LN_EPS) * scale + bias).astype(BF)


def fill(dst, piece_refs, pos_ref, segments):
    at = 0
    for ref, lengths in zip(piece_refs, segments):
        start = 0
        for length in lengths:
            dst[:, pl.ds(pl.multiple_of(pos_ref[at], RB), length), :] = ref[:, start:start + length, :]
            start += length
            at += 1


def proj_kernel(sides, segments, keep, extra, pos_ref, *refs):
    pieces = len(segments)
    z_refs, refs = refs[:pieces], refs[pieces:]
    m_ref, s_ref, b_ref, w_ref = refs[:4]
    refs = refs[4 + extra:]
    outs, refs = refs[:sides], refs[sides:]
    if keep:
        (zn_ref, zfull), refs = refs[:2], refs[2:]
    else:
        zfull, refs = refs[-1], refs[:-1]
    znm, tmp = refs
    rows, n, d = zfull.shape
    ka = znm.shape[1]
    fill(zfull, z_refs, pos_ref, segments)
    ones_row = lax.broadcasted_iota(jnp.int32, (ka - d, LANES), 0) == 0
    unroll = 4

    @pl.loop(0, rows, step=unroll)
    def _(i0):
        for u in range(unroll):
            i = i0 + u
            m = m_ref[pl.ds(i, 1), :]
            for t in range(n // LANES):
                sl = slice(t * LANES, (t + 1) * LANES)
                y = norm_columns(zfull[i, sl, :].T.astype(F32), s_ref[...], b_ref[...])
                if keep:
                    zn_ref[i, sl, :] = y.T
                znm[i, :d, sl] = y * m[:, sl].astype(BF)
                znm[i, d:, sl] = jnp.where(ones_row, jnp.broadcast_to(m[:, sl], ones_row.shape), 0.0).astype(BF)

    parts, half = w_ref.shape[1], w_ref.shape[2] // 2

    @pl.loop(0, rows, unroll=ROWS_AT_ONCE)
    def _(i):
        rhs = znm[i]
        for sd in range(sides):
            for h in range(parts):
                p = jnp.dot(w_ref[sd, h], rhs, preferred_element_type=F32)
                tmp[sd, i, h * half:(h + 1) * half, :] = (jax.nn.sigmoid(p[half:]) * p[:half]).astype(BF)

    @pl.loop(0, parts * half // RB, unroll=2)
    def _(k):
        k0 = pl.multiple_of(k * RB, RB)
        for sd in range(sides):
            outs[sd][pl.ds(k0, RB)] = jnp.transpose(tmp[sd, :, pl.ds(k0, RB), :], (1, 0, 2))


def project(pieces, pos, mask, scale, bias, w, r0, r, total, keep=None, deps=()):
    n = mask.shape[1]
    d = pieces[0][0].shape[2]
    sides, parts, half2, ka = w.shape
    c = parts * half2 // 2
    blk = r0 // RB
    full = sides == 2
    b_shape, b_spec = jax.ShapeDtypeStruct((c, r, n), BF), pl.BlockSpec((c, RB, n), lambda i, pos: (0, i, 0))
    out_shape, out_specs = [b_shape], [b_spec]
    if full:
        out_shape = [jax.ShapeDtypeStruct((c, total, n), BF), b_shape] + [jax.ShapeDtypeStruct((total, n, d), BF)] * 2
        out_specs = [pl.BlockSpec((c, RB, n), lambda i, pos: (0, i + blk, 0)), b_spec] + [pl.BlockSpec((RB, n, d), lambda i, pos: (i + blk, 0, 0))] * 2
    scratch = [pltpu.VMEM((RB, ka, n), BF), pltpu.VMEM((sides, RB, c, n), BF)]
    if not full:
        scratch = scratch + [pltpu.VMEM((RB, n, d), BF)]
    keep = tuple(keep or ())
    extra = keep + tuple(deps)
    count = len(pieces)
    spec = pltpu.PrefetchScalarGridSpec(
        num_scalar_prefetch=1,
        grid=(r // RB,),
        in_specs=[pl.BlockSpec((RB, x.shape[1], d), functools.partial(lambda f, i, pos: (i + f, 0, 0), f // RB)) for x, f, _ in pieces]
        + [
            pl.BlockSpec((RB, n), lambda i, pos: (i + blk, 0)),
            pl.BlockSpec((d, LANES), lambda i, pos: (0, 0)),
            pl.BlockSpec((d, LANES), lambda i, pos: (0, 0)),
            pl.BlockSpec(w.shape, lambda i, pos: (0, 0, 0, 0)),
        ]
        + [ANY] * len(extra),
        out_specs=out_specs,
        scratch_shapes=scratch,
    )
    first = 1 + count + 4
    return pl.pallas_call(
        functools.partial(proj_kernel, sides, [g for _, _, g in pieces], full, len(extra)),
        grid_spec=spec,
        out_shape=out_shape,
        name="project",
        input_output_aliases={first: 0, first + 1: 2, first + 2: 3} if keep else {},
        cost_estimate=pl.CostEstimate(flops=16 * sides * r * n * d * c, bytes_accessed=2 * r * n * d * (2 + sides), transcendentals=0),
        compiler_params=pltpu.CompilerParams(vmem_limit_bytes=VMEM),
    )(pos, *[x for x, _, _ in pieces], mask, scale, bias, w, *extra)


def tri_kernel(nb, cb, widths, split, extra, pos_ref, a_ref, *refs):
    b_refs, refs = refs[:len(widths)], refs[len(widths):]
    z_ref, zn_ref, ls_ref, lb_ref, wo_ref, bo_ref, wg_ref, bg_ref = refs[:8]
    refs = refs[8 + extra:]
    outs, (acc, on, res) = refs[:-3], refs[-3:]
    step = pl.program_id(0)
    c = acc.shape[0]
    width = sum(widths)

    @pl.when(step < nb)
    def _():
        for k in range(cb):
            both = jnp.concatenate([b[k] for b in b_refs], axis=0)
            acc[step * cb + k] = lax.dot_general(a_ref[k], both, (((1,), (1,)), ((), ())), preferred_element_type=F32)

    @pl.when(step >= nb)
    def _():
        ib = pl.multiple_of((step - nb) * RB, RB)
        zero = jnp.zeros((RB, width), F32)

        def block(k):
            return acc[pl.ds(pl.multiple_of(k * RB, RB), RB), pl.ds(ib, RB), :]

        mean = lax.fori_loop(0, c // RB, lambda k, t: t + jnp.sum(block(k), axis=0), zero) * (1.0 / c)

        def squares(k, t):
            v = block(k) - mean[None]
            return t + jnp.sum(v * v, axis=0)

        rstd = lax.rsqrt(lax.fori_loop(0, c // RB, squares, zero) * (1.0 / c) + LN_EPS)

        @pl.loop(0, c // RB)
        def _(k):
            k0 = pl.multiple_of(k * RB, RB)
            v = (block(k) - mean[None]) * rstd[None] * ls_ref[pl.ds(k0, RB), :, :width] + lb_ref[pl.ds(k0, RB), :, :width]
            on[:, pl.ds(k0, RB), :] = jnp.transpose(v.astype(BF), (1, 0, 2))

        g_rows = ROWS_AT_ONCE

        @pl.loop(0, RB, step=g_rows)
        def _(i0):
            rs = pl.ds(i0, g_rows)
            ont = jnp.transpose(on[rs], (0, 2, 1)).reshape(g_rows * width, c)
            u = jnp.dot(ont, wo_ref[...], preferred_element_type=F32) + bo_ref[...]
            u = u.astype(BF).astype(F32).reshape(g_rows, width, -1)
            start = 0
            for h, wd in enumerate(widths):
                at = pl.ds(pl.multiple_of(pos_ref[h], RB), wd)
                g = jnp.dot(zn_ref[rs, at, :].reshape(g_rows * wd, -1), wg_ref[...], preferred_element_type=F32) + bg_ref[...]
                gu = jax.nn.sigmoid(g).reshape(g_rows, wd, -1) * u[:, start:start + wd]
                res[rs, start:start + wd, :] = (z_ref[rs, at, :].astype(F32) + gu).astype(BF)
                start += wd

        if split is None:
            outs[0][...] = res[...]
        else:
            @pl.when(step - nb < split)
            def _():
                outs[0][...] = res[...]

            @pl.when(step - nb >= split)
            def _():
                outs[1][...] = res[...]


def triangle(pos, a, bs, z, zn, tail, split=None, deps=()):
    c, r, n = a.shape
    d = z.shape[2]
    cb = RB
    nb = c // cb
    widths = [b.shape[1] for b in bs]
    width = sum(widths)

    def first(s, pos):
        return jnp.minimum(s, nb - 1), 0, 0

    def later(s):
        return jnp.maximum(s - nb, 0)

    def whole2(s, pos):
        return 0, 0

    def whole3(s, pos):
        return 0, 0, 0

    def rows_of(s, pos):
        return later(s), 0, 0

    if split is None:
        out_shape = [jax.ShapeDtypeStruct((r, width, d), BF)]
        out_specs = [pl.BlockSpec((RB, width, d), rows_of)]
        cut = None
    else:
        cut = split // RB
        out_shape = [jax.ShapeDtypeStruct((k, width, d), BF) for k in (split, r - split)]
        out_specs = [
            pl.BlockSpec((RB, width, d), lambda s, pos: (jnp.minimum(later(s), cut - 1), 0, 0)),
            pl.BlockSpec((RB, width, d), lambda s, pos: (jnp.maximum(later(s) - cut, 0), 0, 0)),
        ]
    spec = pltpu.PrefetchScalarGridSpec(
        num_scalar_prefetch=1,
        grid=(nb + r // RB,),
        in_specs=[pl.BlockSpec((cb, r, n), first)]
        + [pl.BlockSpec((cb, j, n), first) for j in widths]
        + [pl.BlockSpec((RB, n, d), rows_of), pl.BlockSpec((RB, n, d), rows_of)]
        + [pl.BlockSpec(x.shape, whole3 if x.ndim == 3 else whole2) for x in tail]
        + [ANY] * len(deps),
        out_specs=out_specs,
        scratch_shapes=[pltpu.VMEM((c, r, width), F32), pltpu.VMEM((RB, c, width), BF), pltpu.VMEM((RB, width, d), BF)],
    )
    return pl.pallas_call(
        functools.partial(tri_kernel, nb, cb, widths, cut, len(deps)),
        grid_spec=spec,
        out_shape=out_shape,
        name="triangle",
        cost_estimate=pl.CostEstimate(flops=16 * r * n * width * c, bytes_accessed=2 * c * n * (r + width), transcendentals=0),
        compiler_params=pltpu.CompilerParams(vmem_limit_bytes=VMEM),
    )(pos, a, *bs, z, zn, *tail, *deps)


def assemble_kernel(segments, pos_ref, *refs):
    fill(refs[-1], refs[:-1], pos_ref, segments)


def assemble(pieces, pos, n):
    r, _, d = pieces[0][0].shape
    spec = pltpu.PrefetchScalarGridSpec(
        num_scalar_prefetch=1,
        grid=(r // RB,),
        in_specs=[pl.BlockSpec((RB, x.shape[1], d), lambda i, pos: (i, 0, 0)) for x, _ in pieces],
        out_specs=pl.BlockSpec((RB, n, d), lambda i, pos: (i, 0, 0)),
    )
    return pl.pallas_call(
        functools.partial(assemble_kernel, [g for _, g in pieces]),
        grid_spec=spec,
        out_shape=jax.ShapeDtypeStruct((r, n, d), BF),
        name="assemble",
    )(pos, *[x for x, _ in pieces])


def pair_weight(w_pair, b_pair):
    d, c2 = w_pair.shape
    wide = jnp.concatenate([w_pair.T, b_pair[:, None], jnp.zeros((c2, 15), w_pair.dtype)], axis=1)
    value, gate = wide.reshape(2, 2, c2 // 4, d + 16)
    return jnp.concatenate([value, gate], axis=1)


def solution(mesh):
    row_spec = P(('batch', 'dap'), None, None)
    mask_spec = P(('batch', 'dap'), None)
    vec_spec = P(None, None)
    mat_spec = P(None, None, None)
    size = mesh.shape['dap']
    chips = size // 2
    side = [1 - 2 * (i % 2) for i in range(size)]
    to_helper = [(i, (i + 2 * side[i]) % size) for i in range(size)]
    to_other = [(i, (i - 2 * side[i]) % size) for i in range(size)]
    to_partner = [(i, i ^ 1) for i in range(size)]

    def device_fn(z_rows, mask_rows, ln_in_scale, ln_in_bias, w_in, b_in, w_gate, b_gate, ln_out_scale, ln_out_bias, w_out, b_out):
        def send(x, perm):
            return lax.ppermute(x, 'dap', perm)

        layers, d, hidden4 = w_in.shape
        h2 = hidden4 // 2
        rows, n, _ = z_rows.shape
        lo = RB
        hi = rows - lo
        parts = ((0, hi), (hi, lo))
        index = lax.axis_index('dap')
        core, chip = index % 2, index // 2
        sgn = 1 - 2 * core

        def columns(segs, shift=0):
            at = [2 * rows * lax.rem(chip + (k + shift) * sgn + 4 * chips, chips) + rows * jnp.where(flip, 1 - core, core) + r0 for k, flip, r0, _ in segs]
            return jnp.stack(at).astype(jnp.int32)

        def lengths(segs):
            return [g[3] for g in segs]

        def both_cores(k):
            return [(k, flip, r0, r) for r0, r in parts for flip in (0, 1)]

        mid = [[(k, flip, r0, r) for k in (1, -1) for flip in (0, 1)] for r0, r in parts]
        kinds = [both_cores(0), mid[0], mid[1], both_cores(2)]
        every = [g for kind in kinds for g in kind]

        z_hi, z_lo = z_rows[:hi], z_rows[hi:]
        near_in, other_in = [None, None], [None, None]
        near_in[0], other_in[0] = send(z_hi, to_helper), send(z_hi, to_other)
        mask = mask_rows.astype(F32)
        mask_near, mask_other = send(mask, to_helper), send(mask, to_other)
        near_in[1], other_in[1] = send(z_lo, to_helper), send(z_lo, to_other)

        start = jnp.zeros((1,), jnp.int32)
        own_p = [[(z_rows, r0, [n])] for r0, _ in parts]
        near_p = [[(x, 0, [n])] for x in near_in]
        other_p = [[(x, 0, [n])] for x in other_in]
        pos = [start] * 3
        last = ()

        for layer in range(layers):
            w = jnp.stack([pair_weight(w_in[layer, :, :h2], b_in[layer, :h2]), pair_weight(w_in[layer, :, h2:], b_in[layer, h2:])])
            scale = jnp.broadcast_to(ln_in_scale[layer].astype(F32)[:, None], (d, LANES))
            bias = jnp.broadcast_to(ln_in_bias[layer].astype(F32)[:, None], (d, LANES))
            ls = jnp.broadcast_to(ln_out_scale[layer].astype(F32)[:, None, None], (h2 // 2, 1, LANES))
            lb = jnp.broadcast_to(ln_out_bias[layer].astype(F32)[:, None, None], (h2 // 2, 1, LANES))
            tail = (ls, lb, w_out[layer], b_out[layer].astype(F32)[None], w_gate[layer], b_gate[layer].astype(F32)[None])
            final = layer + 1 == layers

            def side_of(pieces, where, m, part, sides, keep, deps):
                r0, r = parts[part]
                return project(pieces, where, m, scale, bias, w[2 - sides:], r0, r, rows, keep, deps)

            b = [None, None]
            b_p = [None, None]
            bn, bn_p, bo, bo_p = [None] * 2, [None] * 2, [None] * 2, [None] * 2
            own = near = None
            for part in (0, 1):
                a_, b[part], zn_, z_ = side_of(own_p[part], pos[0], mask, part, 2, own, last)
                own = (a_, zn_, z_)
                last = (b[part],)
                b_p[part] = send(b[part], to_partner)
                if layer > 0 and part == 0:
                    other_p[1] = other_pieces(1)
            if layer == 0:
                p0, = triangle(columns(kinds[0]), own[0], [b[0], b_p[0], b[1], b_p[1]], own[2], own[1], tail, None, last)
                last = (p0,)
                p0_near, p0_other = send(p0, to_helper), send(p0, to_other)
            for part in (0, 1):
                a_, bn[part], zn_, z_ = side_of(near_p[part], pos[1], mask_near, part, 2, near, last)
                near = (a_, zn_, z_)
                last = (bn[part],)
                bn_p[part] = send(bn[part], to_partner)
                bo[part], = side_of(other_p[part], pos[2], mask_other, part, 1, None, last)
                last = (bo[part],)
                bo_p[part] = send(bo[part], to_partner)
                if part == 0:
                    if layer > 0:
                        p0, = triangle(columns(kinds[0]), own[0], [b[0], b_p[0], b[1], b_p[1]], own[2], own[1], tail, None, last)
                        last = (p0,)
                    c1 = triangle(columns(kinds[1]), own[0], [bo[0], bn_p[0], bn[0], bo_p[0]], own[2], own[1], tail, None if final else hi, last)
                    last = (c1[0],)
                    if not final:
                        c1_near, c1_other = [send(c1[0], to_helper)], [send(c1[0], to_other)]
            far = triangle(columns(kinds[3], -1), near[0], [bo[0], bn_p[0], bo[1], bn_p[1]], near[2], near[1], tail, None if final else hi, last)
            last = (far[0],)
            p3 = [send(x, to_other) for x in far]
            c2 = triangle(columns(kinds[2]), own[0], [bo[1], bn_p[1], bn[1], bo_p[1]], own[2], own[1], tail, None if final else hi, last)
            last = (c2[0],)
            if final:
                return assemble([(x, lengths(g)) for x, g in zip((p0, c1[0], c2[0], p3[0]), kinds)], columns(every), n)

            c2_near, c2_other = [send(c2[0], to_helper)], [send(c2[0], to_other)]
            for got, x in ((c1_near, c1), (c2_near, c2)):
                got.append(send(x[1], to_helper))
            for got, x in ((c1_other, c1), (c2_other, c2)):
                got.append(send(x[1], to_other))

            def group(x0, x1, x2, x3, part):
                return [(x, parts[part][0] if q == 0 else 0, lengths(kinds[q])) for q, x in enumerate((x0, x1, x2, x3))]

            own_p = [group(p0, c1[k], c2[k], p3[k], k) for k in (0, 1)]
            near_p = [group(p0_near, c1_near[k], c2_near[k], far[k], k) for k in (0, 1)]

            def other_pieces(k):
                return group(p0_other, c1_other[k], c2_other[k], send(p3[k], to_other), k)

            other_p = [other_pieces(0), None]
            pos = [columns(every), columns(every, -1), columns(every, 1)]

    return jax.shard_map(device_fn, mesh=mesh, in_specs=(row_spec, mask_spec, vec_spec, vec_spec, mat_spec, vec_spec, mat_spec, vec_spec, vec_spec, vec_spec, mat_spec, vec_spec), out_specs=row_spec, check_vma=False)
```

profile of v0, /device:TPU:113, one launch (start us, length us, event | category | flops | bytes accessed | tf_op | source)
XLA Modules:
  0.0 422.6 jit_solution(525576422071154564)
XLA Ops:
  0.0 1.0 slice_bitcast_fusion.1
  1.0 0.8 slice_bitcast_fusion.9
  1.8 0.8 maximum_maximum_fusion.2
  3.1 1.3 bitcast_convert_fusion.3
  4.3 1.2 bitcast_convert_fusion.2
  5.6 1.5 convert_element_type.99.refs_1_.refs_4_
  7.8 0.7 pad_maximum_fusion.refs_4_
  8.5 0.7 broadcast_in_dim.16.refs_2_
  9.2 0.7 broadcast_in_dim.17.refs_3_
  9.9 14.8 %project.12 = (bf16[128,48,384]{2,1,0:T(8,128)(2,1)}, bf16[128,32,384]{2,1,0:T(8,128)(2,1)}, bf16[48,384,128]{2,1,0:T(8,128)(2,1)}, bf16[48,384,128]{2,1,0:T(8,128)(2,1)}) custom-call(s32[1]{0:T(128)} %constant.156.clone.1.pos_ref, bf16[48,384,128]{2,1,0:T(8,128)(2,1)} %refs_0_.3, f32[48,384]{1,0:T(8,128)} %convert_element_type.99.refs_1_.refs_4_, ...), custom_call_target="tpu_custom_call" | custom-call | flops 6442450944 | bytes 12582912 | tf_op jit(solution)/shard_map/project/pallas_call | solution.py:118
  24.8 0.7 collective-permute-start
  25.5 4.0 slice.98
  29.5 3.6 collective-permute-start.4
  33.1 9.5 %project.13 = (bf16[128,48,384]{2,1,0:T(8,128)(2,1)}, bf16[128,16,384]{2,1,0:T(8,128)(2,1)}, bf16[48,384,128]{2,1,0:T(8,128)(2,1)}, bf16[48,384,128]{2,1,0:T(8,128)(2,1)}) custom-call(s32[1]{0:T(128)} %constant.156.clone.1.pos_ref, bf16[48,384,128]{2,1,0:T(8,128)(2,1)} %refs_0_.3, ...), custom_call_target="tpu_custom_call", output_to_operand_aliasing={{0}: (6, {}), {2}: (7, {}), {3}: (8, {})} | custom-call | flops 3221225472 | bytes 6291456 | tf_op jit(solution)/shard_map/project/pallas_call | solution.py:118
  42.9 2.4 collective-permute-start.5
  45.9 1.3 bitcast_convert_fusion.1
  47.2 1.3 bitcast_convert_fusion
  48.4 1.3 slice_convert_fusion
  49.7 1.5 slice_bitcast_fusion.4
  51.3 0.8 broadcast_in_dim.18.refs_6_
  52.1 0.8 broadcast_in_dim.19.refs_7_
  52.9 16.5 %triangle.8.refs_5_.refs_0_ = bf16[48,96,128]{2,1,0:T(8,128)(2,1)} custom-call(s32[4]{0:T(128)} %pad_add_fusion.pos_ref, bf16[128,48,384]{2,1,0:T(8,128)(2,1)} %get-tuple-element.47.a_ref, bf16[128,32,384]{2,1,0:T(8,128)(2,1)} %get-tuple-element.46.refs_8_.refs_0_, bf16[128,32,384]{2,1,0:T(8,128)(2,1)} %collective-permute-done.refs_1_, ...), custom_call_target="tpu_custom_call" | custom-call | flops 3623878656 | bytes 14155776 | tf_op jit(solution)/shard_map/triangle/pallas_call | solution.py:239
  69.4 33.0 %collective-permute-done.5.refs_1_.refs_4_ = f32[48,384]{1,0:T(8,128)} collective-permute-done((f32[48,384]{1,0:T(8,128)}, f32[48,384]{1,0:T(8,128)}, u32[]{:S(2)}, u32[]{:S(2)}) %collective-permute-start.5) | collective-permute-done | bytes 73760 | tf_op jit(solution)/shard_map/ppermute | solution.py:290
  102.4 14.9 %project.14 = (bf16[128,48,384]{2,1,0:T(8,128)(2,1)}, bf16[128,32,384]{2,1,0:T(8,128)(2,1)}, bf16[48,384,128]{2,1,0:T(8,128)(2,1)}, bf16[48,384,128]{2,1,0:T(8,128)(2,1)}) custom-call(s32[1]{0:T(128)} %constant.156.clone.1.pos_ref, bf16[32,384,128]{2,1,0:T(8,128)(2,1)} %collective-permute-done.4.refs_0_, f32[48,384]{1,0:T(8,128)} %collective-permute-done.5.refs_1_.refs_4_, ...), custom_call_target="tpu_custom_call" | custom-call | flops 6442450944 | bytes 12582912 | tf_op jit(solution)/shard_map/project/pallas_call | solution.py:118
  117.4 9.9 %project.15.refs_0_.refs_12_ = bf16[128,32,384]{2,1,0:T(8,128)(2,1)} custom-call(s32[1]{0:T(128)} %constant.156.clone.1.pos_ref, bf16[32,384,128]{2,1,0:T(8,128)(2,1)} %collective-permute-done.2.refs_0_, f32[48,384]{1,0:T(8,128)} %collective-permute-done.3.refs_1_.refs_4_, f32[128,128]{1,0:T(8,128)} %broadcast_in_dim.16.refs_2_, ...), custom_call_target="tpu_custom_call" | custom-call | flops 3221225472 | bytes 9437184 | tf_op jit(solution)/shard_map/project/pallas_call | solution.py:118
  127.8 2.7 slice.99
  130.5 3.4 collective-permute-start.9
  134.6 3.2 collective-permute-done.6.refs_1_
  137.8 18.5 %triangle.9 = (bf16[32,128,128]{2,1,0:T(8,128)(2,1)}, bf16[16,128,128]{2,1,0:T(8,128)(2,1)}) custom-call(s32[4]{0:T(128)} %pad_add_fusion.1.pos_ref, bf16[128,48,384]{2,1,0:T(8,128)(2,1)} %get-tuple-element.47.a_ref, bf16[128,32,384]{2,1,0:T(8,128)(2,1)} %project.15.refs_0_.refs_12_, bf16[128,32,384]{2,1,0:T(8,128)(2,1)} %collective-permute-done.6.refs_1_, ...), custom_call_target="tpu_custom_call" | custom-call | flops 4831838208 | bytes 17301504 | tf_op jit(solution)/shard_map/triangle/pallas_call | solution.py:239
  156.3 11.7 %collective-permute-done.9.refs_0_ = bf16[16,384,128]{2,1,0:T(8,128)(2,1)} collective-permute-done((bf16[16,384,128]{2,1,0:T(8,128)(2,1)}, bf16[16,384,128]{2,1,0:T(8,128)(2,1)}, u32[]{:S(2)}, u32[]{:S(2)}) %collective-permute-start.9) | collective-permute-done | bytes 1572896 | tf_op jit(solution)/shard_map/ppermute | solution.py:290
  167.9 9.6 %project.16 = (bf16[128,48,384]{2,1,0:T(8,128)(2,1)}, bf16[128,16,384]{2,1,0:T(8,128)(2,1)}, bf16[48,384,128]{2,1,0:T(8,128)(2,1)}, bf16[48,384,128]{2,1,0:T(8,128)(2,1)}) custom-call(s32[1]{0:T(128)} %constant.156.clone.1.pos_ref, bf16[16,384,128]{2,1,0:T(8,128)(2,1)} %collective-permute-done.9.refs_0_, ...), custom_call_target="tpu_custom_call", output_to_operand_aliasing={{0}: (6, {}), {2}: (7, {}), {3}: (8, {})} | custom-call | flops 3221225472 | bytes 6291456 | tf_op jit(solution)/shard_map/project/pallas_call | solution.py:118
  177.5 6.2 %project.17.refs_2_.refs_12_.refs_0_ = bf16[128,16,384]{2,1,0:T(8,128)(2,1)} custom-call(s32[1]{0:T(128)} %constant.156.clone.1.pos_ref, bf16[16,384,128]{2,1,0:T(8,128)(2,1)} %collective-permute-done.8.refs_0_, f32[48,384]{1,0:T(8,128)} %collective-permute-done.3.refs_1_.refs_4_, f32[128,128]{1,0:T(8,128)} %broadcast_in_dim.16.refs_2_, ...), custom_call_target="tpu_custom_call" | custom-call | flops 1610612736 | bytes 4718592 | tf_op jit(solution)/shard_map/project/pallas_call | solution.py:118
  184.8 3.4 collective-permute-start.20
  188.2 16.7 %triangle.10 = (bf16[32,96,128]{2,1,0:T(8,128)(2,1)}, bf16[16,96,128]{2,1,0:T(8,128)(2,1)}) custom-call(s32[4]{0:T(128)} %pad_add_fusion.4.pos_ref, bf16[128,48,384]{2,1,0:T(8,128)(2,1)} %get-tuple-element.58.a_ref, bf16[128,32,384]{2,1,0:T(8,128)(2,1)} %project.15.refs_0_.refs_12_, bf16[128,32,384]{2,1,0:T(8,128)(2,1)} %collective-permute-done.6.refs_1_, ...), custom_call_target="tpu_custom_call" | custom-call | flops 3623878656 | bytes 14155776 | tf_op jit(solution)/shard_map/triangle/pallas_call | solution.py:239
  205.0 0.8 fusion
  209.7 0.8 pad_maximum_fusion.1.refs_7_
  210.4 2.7 collective-permute-start.21
  213.1 15.1 %triangle.11 = (bf16[32,64,128]{2,1,0:T(8,128)(2,1)}, bf16[16,64,128]{2,1,0:T(8,128)(2,1)}) custom-call(s32[4]{0:T(128)} %pad_add_fusion.3.pos_ref, bf16[128,48,384]{2,1,0:T(8,128)(2,1)} %get-tuple-element.47.a_ref, bf16[128,16,384]{2,1,0:T(8,128)(2,1)} %project.17.refs_2_.refs_12_.refs_0_, bf16[128,16,384]{2,1,0:T(8,128)(2,1)} %collective-permute-done.10.refs_3_.refs_1_, ...), custom_call_target="tpu_custom_call" | custom-call | flops 2415919104 | bytes 11010048 | tf_op jit(solution)/shard_map/triangle/pallas_call | solution.py:239
  228.2 0.9 collective-permute-start.12
  229.1 2.0 collective-permute-start.22
  231.1 1.3 broadcast_in_dim.20.refs_5_
  232.4 1.3 broadcast_in_dim.21.refs_6_
  233.7 15.9 %project.18 = (bf16[128,48,384]{2,1,0:T(8,128)(2,1)}, bf16[128,32,384]{2,1,0:T(8,128)(2,1)}, bf16[48,384,128]{2,1,0:T(8,128)(2,1)}, bf16[48,384,128]{2,1,0:T(8,128)(2,1)}) custom-call(s32[16]{0:T(128)} %stack.90.pos_ref, bf16[48,96,128]{2,1,0:T(8,128)(2,1)} %triangle.8.refs_5_.refs_0_, bf16[32,128,128]{2,1,0:T(8,128)(2,1)} %get-tuple-element.56.refs_8_.refs_1_, ...), custom_call_target="tpu_custom_call" | custom-call | flops 6442450944 | bytes 12582912 | tf_op jit(solution)/shard_map/project/pallas_call | solution.py:118
  249.6 12.7 %collective-permute-done.12.refs_3_ = bf16[16,96,128]{2,1,0:T(8,128)(2,1)} collective-permute-done((bf16[16,96,128]{2,1,0:T(8,128)(2,1)}, bf16[16,96,128]{2,1,0:T(8,128)(2,1)}, u32[]{:S(2)}, u32[]{:S(2)}) %collective-permute-start.12) | collective-permute-done | bytes 393248 | tf_op jit(solution)/shard_map/ppermute | solution.py:290
  262.3 10.2 %project.19 = (bf16[128,48,384]{2,1,0:T(8,128)(2,1)}, bf16[128,16,384]{2,1,0:T(8,128)(2,1)}, bf16[48,384,128]{2,1,0:T(8,128)(2,1)}, bf16[48,384,128]{2,1,0:T(8,128)(2,1)}) custom-call(s32[16]{0:T(128)} %stack.90.pos_ref, bf16[48,96,128]{2,1,0:T(8,128)(2,1)} %triangle.8.refs_5_.refs_0_, ...), custom_call_target="tpu_custom_call", output_to_operand_aliasing={{0}: (9, {}), {2}: (10, {}), {3}: (11, {})} | custom-call | flops 3221225472 | bytes 6291456 | tf_op jit(solution)/shard_map/project/pallas_call | solution.py:118
  272.6 2.2 collective-permute-start.14
  274.8 16.2 %project.20 = (bf16[128,48,384]{2,1,0:T(8,128)(2,1)}, bf16[128,32,384]{2,1,0:T(8,128)(2,1)}, bf16[48,384,128]{2,1,0:T(8,128)(2,1)}, bf16[48,384,128]{2,1,0:T(8,128)(2,1)}) custom-call(s32[16]{0:T(128)} %stack.110.pos_ref, bf16[48,96,128]{2,1,0:T(8,128)(2,1)} %collective-permute-done.20.refs_0_, bf16[32,128,128]{2,1,0:T(8,128)(2,1)} %collective-permute-done.21.refs_1_, ...), custom_call_target="tpu_custom_call" | custom-call | flops 6442450944 | bytes 12582912 | tf_op jit(solution)/shard_map/project/pallas_call | solution.py:118
  291.0 11.0 %project.21.refs_12_.refs_0_ = bf16[128,32,384]{2,1,0:T(8,128)(2,1)} custom-call(s32[16]{0:T(128)} %stack.105.pos_ref, bf16[48,96,128]{2,1,0:T(8,128)(2,1)} %collective-permute-done.16.refs_0_, bf16[32,128,128]{2,1,0:T(8,128)(2,1)} %collective-permute-done.17.refs_1_, bf16[32,64,128]{2,1,0:T(8,128)(2,1)} %collective-permute-done.18.refs_2_, ...), custom_call_target="tpu_custom_call" | custom-call | flops 3221225472 | bytes 9437184 | tf_op jit(solution)/shard_map/project/pallas_call | solution.py:118
  302.5 1.0 collective-permute-start.28
  303.5 6.8 %collective-permute-done.15.refs_3_ = bf16[128,16,384]{2,1,0:T(8,128)(2,1)} collective-permute-done((bf16[128,16,384]{2,1,0:T(8,128)(2,1)}, bf16[128,16,384]{2,1,0:T(8,128)(2,1)}, u32[]{:S(2)}, u32[]{:S(2)}) %collective-permute-start.15) | collective-permute-done | bytes 1572896 | tf_op jit(solution)/shard_map/ppermute | solution.py:290
  310.3 0.9 collective-permute-start.29
  311.3 1.5 broadcast_in_dim.22.refs_6_
  312.7 1.4 broadcast_in_dim.23.refs_7_
  314.2 16.6 %triangle.12.refs_12_.refs_0_ = bf16[48,96,128]{2,1,0:T(8,128)(2,1)} custom-call(s32[4]{0:T(128)} %pad_add_fusion.pos_ref, bf16[128,48,384]{2,1,0:T(8,128)(2,1)} %get-tuple-element.69.a_ref, bf16[128,32,384]{2,1,0:T(8,128)(2,1)} %get-tuple-element.68.refs_11_.refs_0_, bf16[128,32,384]{2,1,0:T(8,128)(2,1)} %collective-permute-done.14.refs_1_, ...), custom_call_target="tpu_custom_call" | custom-call | flops 3623878656 | bytes 14155776 | tf_op jit(solution)/shard_map/triangle/pallas_call | solution.py:239
  330.8 18.2 %triangle.13.refs_11_.refs_1_ = bf16[48,128,128]{2,1,0:T(8,128)(2,1)} custom-call(s32[4]{0:T(128)} %pad_add_fusion.1.pos_ref, bf16[128,48,384]{2,1,0:T(8,128)(2,1)} %get-tuple-element.69.a_ref, bf16[128,32,384]{2,1,0:T(8,128)(2,1)} %project.21.refs_12_.refs_0_, bf16[128,32,384]{2,1,0:T(8,128)(2,1)} %collective-permute-done.23.refs_1_, ...), custom_call_target="tpu_custom_call" | custom-call | flops 4831838208 | bytes 17301504 | tf_op jit(solution)/shard_map/triangle/pallas_call | solution.py:239
  349.0 10.2 %project.22 = (bf16[128,48,384]{2,1,0:T(8,128)(2,1)}, bf16[128,16,384]{2,1,0:T(8,128)(2,1)}, bf16[48,384,128]{2,1,0:T(8,128)(2,1)}, bf16[48,384,128]{2,1,0:T(8,128)(2,1)}) custom-call(s32[16]{0:T(128)} %stack.110.pos_ref, bf16[48,96,128]{2,1,0:T(8,128)(2,1)} %collective-permute-done.20.refs_0_, ...), custom_call_target="tpu_custom_call", output_to_operand_aliasing={{0}: (9, {}), {2}: (10, {}), {3}: (11, {})} | custom-call | flops 3221225472 | bytes 6291456 | tf_op jit(solution)/shard_map/project/pallas_call | solution.py:118
  360.7 1.7 collective-permute-start.26
  362.5 7.0 %collective-permute-done.25.refs_1_ = bf16[16,128,128]{2,1,0:T(8,128)(2,1)} collective-permute-done((bf16[16,128,128]{2,1,0:T(8,128)(2,1)}, bf16[16,128,128]{2,1,0:T(8,128)(2,1)}, u32[]{:S(2)}, u32[]{:S(2)}) %collective-permute-start.25) | collective-permute-done | bytes 524320 | tf_op jit(solution)/shard_map/ppermute | solution.py:290
  369.4 7.0 %collective-permute-done.26.refs_2_ = bf16[16,64,128]{2,1,0:T(8,128)(2,1)} collective-permute-done((bf16[16,64,128]{2,1,0:T(8,128)(2,1)}, bf16[16,64,128]{2,1,0:T(8,128)(2,1)}, u32[]{:S(2)}, u32[]{:S(2)}) %collective-permute-start.26) | collective-permute-done | bytes 262176 | tf_op jit(solution)/shard_map/ppermute | solution.py:290
  376.4 6.9 %project.23.refs_2_.refs_12_.refs_0_ = bf16[128,16,384]{2,1,0:T(8,128)(2,1)} custom-call(s32[16]{0:T(128)} %stack.105.pos_ref, bf16[48,96,128]{2,1,0:T(8,128)(2,1)} %collective-permute-done.16.refs_0_, bf16[16,128,128]{2,1,0:T(8,128)(2,1)} %collective-permute-done.25.refs_1_, bf16[16,64,128]{2,1,0:T(8,128)(2,1)} %collective-permute-done.26.refs_2_, ...), custom_call_target="tpu_custom_call" | custom-call | flops 1610612736 | bytes 4718592 | tf_op jit(solution)/shard_map/project/pallas_call | solution.py:118
  383.3 16.5 %triangle.14.refs_12_ = bf16[48,96,128]{2,1,0:T(8,128)(2,1)} custom-call(s32[4]{0:T(128)} %pad_add_fusion.4.pos_ref, bf16[128,48,384]{2,1,0:T(8,128)(2,1)} %get-tuple-element.78.a_ref, bf16[128,32,384]{2,1,0:T(8,128)(2,1)} %project.21.refs_12_.refs_0_, bf16[128,32,384]{2,1,0:T(8,128)(2,1)} %collective-permute-done.23.refs_1_, ...), custom_call_target="tpu_custom_call" | custom-call | flops 3623878656 | bytes 14155776 | tf_op jit(solution)/shard_map/triangle/pallas_call | solution.py:239
  400.3 14.9 %triangle.15.refs_2_ = bf16[48,64,128]{2,1,0:T(8,128)(2,1)} custom-call(s32[4]{0:T(128)} %pad_add_fusion.3.pos_ref, bf16[128,48,384]{2,1,0:T(8,128)(2,1)} %get-tuple-element.69.a_ref, bf16[128,16,384]{2,1,0:T(8,128)(2,1)} %project.23.refs_2_.refs_12_.refs_0_, bf16[128,16,384]{2,1,0:T(8,128)(2,1)} %collective-permute-done.30.refs_3_.refs_1_, ...), custom_call_target="tpu_custom_call" | custom-call | flops 2415919104 | bytes 11010048 | tf_op jit(solution)/shard_map/triangle/pallas_call | solution.py:239
  415.1 1.5 collective-permute-done.32.refs_3_
  416.6 6.0 %assemble.1 = bf16[48,384,128]{2,1,0:T(8,128)(2,1)} custom-call(s32[16]{0:T(128)} %stack.90.pos_ref, bf16[48,96,128]{2,1,0:T(8,128)(2,1)} %triangle.12.refs_12_.refs_0_, bf16[48,128,128]{2,1,0:T(8,128)(2,1)} %triangle.13.refs_11_.refs_1_, bf16[48,64,128]{2,1,0:T(8,128)(2,1)} %triangle.15.refs_2_, bf16[48,96,128]{2,1,0:T(8,128)(2,1)} %collective-permute-done.32.refs_3_), custom_call_target="tpu_custom_call" | custom-call | tf_op jit(solution)/shard_map/assemble/pallas_call | solution.py:261
  (72 shorter events, 10.8 us)
Async XLA Ops:
  7.1 0.7 copy-start
  24.8 26.5 %collective-permute-start = (bf16[128,32,384]{2,1,0:T(8,128)(2,1)}, bf16[128,32,384]{2,1,0:T(8,128)(2,1)}, u32[]{:S(2)}, u32[]{:S(2)}) collective-permute-start(bf16[128,32,384]{2,1,0:T(8,128)(2,1)} %get-tuple-element.46.refs_8_.refs_0_), channel_id=1, source_target_pairs={{0,1},{1,0},{2,3},{3,2},{4,5},{5,4},{6,7},{7,6},{8,9},{9,8},{10,11... | collective-permute-start | bytes 9437192 | tf_op jit(solution)/shard_map/ppermute | solution.py:290
  29.5 73.0 %collective-permute-start.4 = (bf16[32,384,128]{2,1,0:T(8,128)(2,1)}, bf16[32,384,128]{2,1,0:T(8,128)(2,1)}, u32[]{:S(2)}, u32[]{:S(2)}) collective-permute-start(bf16[32,384,128]{2,1,0:T(8,128)(2,1)} %slice.98), channel_id=1, source_target_pairs={{0,2},{1,7},{2,4},{3,1},{4,6},{5,3},{6,0},{7,5},{8,10},{9,15},{10,... | collective-permute-start | bytes 9437192 | tf_op jit(solution)/shard_map/ppermute | solution.py:290
  33.1 84.3 %collective-permute-start.2 = (bf16[32,384,128]{2,1,0:T(8,128)(2,1)}, bf16[32,384,128]{2,1,0:T(8,128)(2,1)}, u32[]{:S(2)}, u32[]{:S(2)}) collective-permute-start(bf16[32,384,128]{2,1,0:T(8,128)(2,1)} %slice.98), channel_id=1, source_target_pairs={{0,6},{1,3},{2,0},{3,5},{4,2},{5,7},{6,4},{7,1},{8,14},{9,11},{10,... | collective-permute-start | bytes 9437192 | tf_op jit(solution)/shard_map/ppermute | solution.py:290
  42.6 8.6 %collective-permute-start.1 = (bf16[128,16,384]{2,1,0:T(8,128)(2,1)}, bf16[128,16,384]{2,1,0:T(8,128)(2,1)}, u32[]{:S(2)}, u32[]{:S(2)}) collective-permute-start(bf16[128,16,384]{2,1,0:T(8,128)(2,1)} %get-tuple-element.48.refs_2_.refs_12_), channel_id=1, source_target_pairs={{0,1},{1,0},{2,3},{3,2},{4,5},{5,4},{6,7},{7,6},{8,9},{9,8},{10,11... | collective-permute-start | bytes 4718600 | tf_op jit(solution)/shard_map/ppermute | solution.py:290
  42.9 59.6 %collective-permute-start.5 = (f32[48,384]{1,0:T(8,128)}, f32[48,384]{1,0:T(8,128)}, u32[]{:S(2)}, u32[]{:S(2)}) collective-permute-start(f32[48,384]{1,0:T(8,128)} %convert_element_type.99.refs_1_.refs_4_), channel_id=1, source_target_pairs={{0,2},{1,7},{2,4},{3,1},{4,6},{5,3},{6,0},{7,5},{8,10},{9,15},{10,... | collective-permute-start | bytes 221192 | tf_op jit(solution)/shard_map/ppermute | solution.py:290
  51.2 66.2 %collective-permute-start.3 = (f32[48,384]{1,0:T(8,128)}, f32[48,384]{1,0:T(8,128)}, u32[]{:S(2)}, u32[]{:S(2)}) collective-permute-start(f32[48,384]{1,0:T(8,128)} %convert_element_type.99.refs_1_.refs_4_), channel_id=1, source_target_pairs={{0,6},{1,3},{2,0},{3,5},{4,2},{5,7},{6,4},{7,1},{8,14},{9,11},{10,... | collective-permute-start | bytes 221192 | tf_op jit(solution)/shard_map/ppermute | solution.py:290
  127.3 7.3 %collective-permute-start.7 = (bf16[128,32,384]{2,1,0:T(8,128)(2,1)}, bf16[128,32,384]{2,1,0:T(8,128)(2,1)}, u32[]{:S(2)}, u32[]{:S(2)}) collective-permute-start(bf16[128,32,384]{2,1,0:T(8,128)(2,1)} %project.15.refs_0_.refs_12_), channel_id=1, source_target_pairs={{0,1},{1,0},{2,3},{3,2},{4,5},{5,4},{6,7},{7,6},{8,9},{9,8},{10,11... | collective-permute-start | bytes 9437192 | tf_op jit(solution)/shard_map/ppermute | solution.py:290
  127.3 10.5 %collective-permute-start.6 = (bf16[128,32,384]{2,1,0:T(8,128)(2,1)}, bf16[128,32,384]{2,1,0:T(8,128)(2,1)}, u32[]{:S(2)}, u32[]{:S(2)}) collective-permute-start(bf16[128,32,384]{2,1,0:T(8,128)(2,1)} %get-tuple-element.51.refs_5_.refs_2_), channel_id=1, source_target_pairs={{0,1},{1,0},{2,3},{3,2},{4,5},{5,4},{6,7},{7,6},{8,9},{9,8},{10,11... | collective-permute-start | bytes 9437192 | tf_op jit(solution)/shard_map/ppermute | solution.py:290
  130.5 37.4 %collective-permute-start.9 = (bf16[16,384,128]{2,1,0:T(8,128)(2,1)}, bf16[16,384,128]{2,1,0:T(8,128)(2,1)}, u32[]{:S(2)}, u32[]{:S(2)}) collective-permute-start(bf16[16,384,128]{2,1,0:T(8,128)(2,1)} %slice.99), channel_id=1, source_target_pairs={{0,2},{1,7},{2,4},{3,1},{4,6},{5,3},{6,0},{7,5},{8,10},{9,15},{10,... | collective-permute-start | bytes 4718600 | tf_op jit(solution)/shard_map/ppermute | solution.py:290
  133.9 43.6 %collective-permute-start.8 = (bf16[16,384,128]{2,1,0:T(8,128)(2,1)}, bf16[16,384,128]{2,1,0:T(8,128)(2,1)}, u32[]{:S(2)}, u32[]{:S(2)}) collective-permute-start(bf16[16,384,128]{2,1,0:T(8,128)(2,1)} %slice.99), channel_id=1, source_target_pairs={{0,6},{1,3},{2,0},{3,5},{4,2},{5,7},{6,4},{7,1},{8,14},{9,11},{10,... | collective-permute-start | bytes 4718600 | tf_op jit(solution)/shard_map/ppermute | solution.py:290
  177.5 10.8 %collective-permute-start.10 = (bf16[128,16,384]{2,1,0:T(8,128)(2,1)}, bf16[128,16,384]{2,1,0:T(8,128)(2,1)}, u32[]{:S(2)}, u32[]{:S(2)}) collective-permute-start(bf16[128,16,384]{2,1,0:T(8,128)(2,1)} %get-tuple-element.57.refs_5_.refs_2_), channel_id=1, source_target_pairs={{0,1},{1,0},{2,3},{3,2},{4,5},{5,4},{6,7},{7,6},{8,9},{9,8},{10,11... | collective-permute-start | bytes 4718600 | tf_op jit(solution)/shard_map/ppermute | solution.py:290
  183.7 29.4 %collective-permute-start.11 = (bf16[128,16,384]{2,1,0:T(8,128)(2,1)}, bf16[128,16,384]{2,1,0:T(8,128)(2,1)}, u32[]{:S(2)}, u32[]{:S(2)}) collective-permute-start(bf16[128,16,384]{2,1,0:T(8,128)(2,1)} %project.17.refs_2_.refs_12_.refs_0_), channel_id=1, source_target_pairs={{0,1},{1,0},{2,3},{3,2},{4,5},{5,4},{6,7},{7,6},{8,9},{9,8},{10,11... | collective-permute-start | bytes 4718600 | tf_op jit(solution)/shard_map/ppermute | solution.py:290
  184.8 43.4 %collective-permute-start.20 = (bf16[48,96,128]{2,1,0:T(8,128)(2,1)}, bf16[48,96,128]{2,1,0:T(8,128)(2,1)}, u32[]{:S(2)}, u32[]{:S(2)}) collective-permute-start(bf16[48,96,128]{2,1,0:T(8,128)(2,1)} %triangle.8.refs_5_.refs_0_), channel_id=1, source_target_pairs={{0,2},{1,7},{2,4},{3,1},{4,6},{5,3},{6,0},{7,5},{8,10},{9,15},{10,... | collective-permute-start | bytes 3538952 | tf_op jit(solution)/shard_map/ppermute | solution.py:290
  204.9 24.2 %collective-permute-start.13 = (bf16[32,96,128]{2,1,0:T(8,128)(2,1)}, bf16[32,96,128]{2,1,0:T(8,128)(2,1)}, u32[]{:S(2)}, u32[]{:S(2)}) collective-permute-start(bf16[32,96,128]{2,1,0:T(8,128)(2,1)} %get-tuple-element.61.refs_12_.refs_3_), channel_id=1, source_target_pairs={{0,6},{1,3},{2,0},{3,5},{4,2},{5,7},{6,4},{7,1},{8,14},{9,11},{10,... | collective-permute-start | bytes 2359304 | tf_op jit(solution)/shard_map/ppermute | solution.py:290
  209.0 0.7 copy-start.1
  210.4 80.5 %collective-permute-start.16 = (bf16[48,96,128]{2,1,0:T(8,128)(2,1)}, bf16[48,96,128]{2,1,0:T(8,128)(2,1)}, u32[]{:S(2)}, u32[]{:S(2)}) collective-permute-start(bf16[48,96,128]{2,1,0:T(8,128)(2,1)} %triangle.8.refs_5_.refs_0_), channel_id=1, source_target_pairs={{0,6},{1,3},{2,0},{3,5},{4,2},{5,7},{6,4},{7,1},{8,14},{9,11},{10,... | collective-permute-start | bytes 3538952 | tf_op jit(solution)/shard_map/ppermute | solution.py:290
  210.4 62.1 %collective-permute-start.21 = (bf16[32,128,128]{2,1,0:T(8,128)(2,1)}, bf16[32,128,128]{2,1,0:T(8,128)(2,1)}, u32[]{:S(2)}, u32[]{:S(2)}) collective-permute-start(bf16[32,128,128]{2,1,0:T(8,128)(2,1)} %get-tuple-element.56.refs_8_.refs_1_), channel_id=1, source_target_pairs={{0,2},{1,7},{2,4},{3,1},{4,6},{5,3},{6,0},{7,5},{8,10},{9,15},{10,... | collective-permute-start | bytes 3145736 | tf_op jit(solution)/shard_map/ppermute | solution.py:290
  213.1 77.9 %collective-permute-start.17 = (bf16[32,128,128]{2,1,0:T(8,128)(2,1)}, bf16[32,128,128]{2,1,0:T(8,128)(2,1)}, u32[]{:S(2)}, u32[]{:S(2)}) collective-permute-start(bf16[32,128,128]{2,1,0:T(8,128)(2,1)} %get-tuple-element.56.refs_8_.refs_1_), channel_id=1, source_target_pairs={{0,6},{1,3},{2,0},{3,5},{4,2},{5,7},{6,4},{7,1},{8,14},{9,11},{10,... | collective-permute-start | bytes 3145736 | tf_op jit(solution)/shard_map/ppermute | solution.py:290
  228.2 34.1 %collective-permute-start.12 = (bf16[16,96,128]{2,1,0:T(8,128)(2,1)}, bf16[16,96,128]{2,1,0:T(8,128)(2,1)}, u32[]{:S(2)}, u32[]{:S(2)}) collective-permute-start(bf16[16,96,128]{2,1,0:T(8,128)(2,1)} %get-tuple-element.63.refs_3_), channel_id=1, source_target_pairs={{0,6},{1,3},{2,0},{3,5},{4,2},{5,7},{6,4},{7,1},{8,14},{9,11},{10,... | collective-permute-start | bytes 1179656 | tf_op jit(solution)/shard_map/ppermute | solution.py:290
  229.1 43.4 %collective-permute-start.22 = (bf16[32,64,128]{2,1,0:T(8,128)(2,1)}, bf16[32,64,128]{2,1,0:T(8,128)(2,1)}, u32[]{:S(2)}, u32[]{:S(2)}) collective-permute-start(bf16[32,64,128]{2,1,0:T(8,128)(2,1)} %get-tuple-element.64.refs_2_.refs_8_), channel_id=1, source_target_pairs={{0,2},{1,7},{2,4},{3,1},{4,6},{5,3},{6,0},{7,5},{8,10},{9,15},{10,... | collective-permute-start | bytes 1572872 | tf_op jit(solution)/shard_map/ppermute | solution.py:290
  262.3 28.7 %collective-permute-start.19 = (bf16[32,96,128]{2,1,0:T(8,128)(2,1)}, bf16[32,96,128]{2,1,0:T(8,128)(2,1)}, u32[]{:S(2)}, u32[]{:S(2)}) collective-permute-start(bf16[32,96,128]{2,1,0:T(8,128)(2,1)} %collective-permute-done.13.refs_3_), channel_id=1, source_target_pairs={{0,6},{1,3},{2,0},{3,5},{4,2},{5,7},{6,4},{7,1},{8,14},{9,11},{10,... | collective-permute-start | bytes 2359304 | tf_op jit(solution)/shard_map/ppermute | solution.py:290
  272.5 18.5 %collective-permute-start.18 = (bf16[32,64,128]{2,1,0:T(8,128)(2,1)}, bf16[32,64,128]{2,1,0:T(8,128)(2,1)}, u32[]{:S(2)}, u32[]{:S(2)}) collective-permute-start(bf16[32,64,128]{2,1,0:T(8,128)(2,1)} %get-tuple-element.64.refs_2_.refs_8_), channel_id=1, source_target_pairs={{0,6},{1,3},{2,0},{3,5},{4,2},{5,7},{6,4},{7,1},{8,14},{9,11},{10,... | collective-permute-start | bytes 1572872 | tf_op jit(solution)/shard_map/ppermute | solution.py:290
  272.6 38.7 %collective-permute-start.14 = (bf16[128,32,384]{2,1,0:T(8,128)(2,1)}, bf16[128,32,384]{2,1,0:T(8,128)(2,1)}, u32[]{:S(2)}, u32[]{:S(2)}) collective-permute-start(bf16[128,32,384]{2,1,0:T(8,128)(2,1)} %get-tuple-element.68.refs_11_.refs_0_), channel_id=1, source_target_pairs={{0,1},{1,0},{2,3},{3,2},{4,5},{5,4},{6,7},{7,6},{8,9},{9,8},{10,11... | collective-permute-start | bytes 9437192 | tf_op jit(solution)/shard_map/ppermute | solution.py:290
  290.9 39.9 %collective-permute-start.23 = (bf16[128,32,384]{2,1,0:T(8,128)(2,1)}, bf16[128,32,384]{2,1,0:T(8,128)(2,1)}, u32[]{:S(2)}, u32[]{:S(2)}) collective-permute-start(bf16[128,32,384]{2,1,0:T(8,128)(2,1)} %get-tuple-element.73.refs_8_.refs_2_), channel_id=1, source_target_pairs={{0,1},{1,0},{2,3},{3,2},{4,5},{5,4},{6,7},{7,6},{8,9},{9,8},{10,11... | collective-permute-start | bytes 9437192 | tf_op jit(solution)/shard_map/ppermute | solution.py:290
  302.0 28.7 %collective-permute-start.24 = (bf16[128,32,384]{2,1,0:T(8,128)(2,1)}, bf16[128,32,384]{2,1,0:T(8,128)(2,1)}, u32[]{:S(2)}, u32[]{:S(2)}) collective-permute-start(bf16[128,32,384]{2,1,0:T(8,128)(2,1)} %project.21.refs_12_.refs_0_), channel_id=1, source_target_pairs={{0,1},{1,0},{2,3},{3,2},{4,5},{5,4},{6,7},{7,6},{8,9},{9,8},{10,11... | collective-permute-start | bytes 9437192 | tf_op jit(solution)/shard_map/ppermute | solution.py:290
  302.5 7.9 %collective-permute-start.15 = (bf16[128,16,384]{2,1,0:T(8,128)(2,1)}, bf16[128,16,384]{2,1,0:T(8,128)(2,1)}, u32[]{:S(2)}, u32[]{:S(2)}) collective-permute-start(bf16[128,16,384]{2,1,0:T(8,128)(2,1)} %get-tuple-element.70.refs_8_.refs_2_), channel_id=1, source_target_pairs={{0,1},{1,0},{2,3},{3,2},{4,5},{5,4},{6,7},{7,6},{8,9},{9,8},{10,11... | collective-permute-start | bytes 4718600 | tf_op jit(solution)/shard_map/ppermute | solution.py:290
  302.5 46.5 %collective-permute-start.28 = (bf16[16,128,128]{2,1,0:T(8,128)(2,1)}, bf16[16,128,128]{2,1,0:T(8,128)(2,1)}, u32[]{:S(2)}, u32[]{:S(2)}) collective-permute-start(bf16[16,128,128]{2,1,0:T(8,128)(2,1)} %get-tuple-element.52.refs_1_), channel_id=1, source_target_pairs={{0,2},{1,7},{2,4},{3,1},{4,6},{5,3},{6,0},{7,5},{8,10},{9,15},{10,... | collective-permute-start | bytes 1572872 | tf_op jit(solution)/shard_map/ppermute | solution.py:290
  310.3 38.7 %collective-permute-start.29 = (bf16[16,64,128]{2,1,0:T(8,128)(2,1)}, bf16[16,64,128]{2,1,0:T(8,128)(2,1)}, u32[]{:S(2)}, u32[]{:S(2)}) collective-permute-start(bf16[16,64,128]{2,1,0:T(8,128)(2,1)} %get-tuple-element.62.refs_2_), channel_id=1, source_target_pairs={{0,2},{1,7},{2,4},{3,1},{4,6},{5,3},{6,0},{7,5},{8,10},{9,15},{10,... | collective-permute-start | bytes 786440 | tf_op jit(solution)/shard_map/ppermute | solution.py:290
  359.2 24.1 %collective-permute-start.30 = (bf16[128,16,384]{2,1,0:T(8,128)(2,1)}, bf16[128,16,384]{2,1,0:T(8,128)(2,1)}, u32[]{:S(2)}, u32[]{:S(2)}) collective-permute-start(bf16[128,16,384]{2,1,0:T(8,128)(2,1)} %get-tuple-element.77.refs_8_.refs_2_), channel_id=1, source_target_pairs={{0,1},{1,0},{2,3},{3,2},{4,5},{5,4},{6,7},{7,6},{8,9},{9,8},{10,11... | collective-permute-start | bytes 4718600 | tf_op jit(solution)/shard_map/ppermute | solution.py:290
  359.9 9.6 %collective-permute-start.25 = (bf16[16,128,128]{2,1,0:T(8,128)(2,1)}, bf16[16,128,128]{2,1,0:T(8,128)(2,1)}, u32[]{:S(2)}, u32[]{:S(2)}) collective-permute-start(bf16[16,128,128]{2,1,0:T(8,128)(2,1)} %get-tuple-element.52.refs_1_), channel_id=1, source_target_pairs={{0,6},{1,3},{2,0},{3,5},{4,2},{5,7},{6,4},{7,1},{8,14},{9,11},{10,... | collective-permute-start | bytes 1572872 | tf_op jit(solution)/shard_map/ppermute | solution.py:290
  360.4 16.1 %collective-permute-start.27 = (bf16[16,96,128]{2,1,0:T(8,128)(2,1)}, bf16[16,96,128]{2,1,0:T(8,128)(2,1)}, u32[]{:S(2)}, u32[]{:S(2)}) collective-permute-start(bf16[16,96,128]{2,1,0:T(8,128)(2,1)} %collective-permute-done.12.refs_3_), channel_id=1, source_target_pairs={{0,6},{1,3},{2,0},{3,5},{4,2},{5,7},{6,4},{7,1},{8,14},{9,11},{10,... | collective-permute-start | bytes 1179656 | tf_op jit(solution)/shard_map/ppermute | solution.py:290
  360.7 15.7 %collective-permute-start.26 = (bf16[16,64,128]{2,1,0:T(8,128)(2,1)}, bf16[16,64,128]{2,1,0:T(8,128)(2,1)}, u32[]{:S(2)}, u32[]{:S(2)}) collective-permute-start(bf16[16,64,128]{2,1,0:T(8,128)(2,1)} %get-tuple-element.62.refs_2_), channel_id=1, source_target_pairs={{0,6},{1,3},{2,0},{3,5},{4,2},{5,7},{6,4},{7,1},{8,14},{9,11},{10,... | collective-permute-start | bytes 786440 | tf_op jit(solution)/shard_map/ppermute | solution.py:290
  383.3 16.9 %collective-permute-start.31 = (bf16[128,16,384]{2,1,0:T(8,128)(2,1)}, bf16[128,16,384]{2,1,0:T(8,128)(2,1)}, u32[]{:S(2)}, u32[]{:S(2)}) collective-permute-start(bf16[128,16,384]{2,1,0:T(8,128)(2,1)} %project.23.refs_2_.refs_12_.refs_0_), channel_id=1, source_target_pairs={{0,1},{1,0},{2,3},{3,2},{4,5},{5,4},{6,7},{7,6},{8,9},{9,8},{10,11... | collective-permute-start | bytes 4718600 | tf_op jit(solution)/shard_map/ppermute | solution.py:290
  399.8 16.8 %collective-permute-start.32 = (bf16[48,96,128]{2,1,0:T(8,128)(2,1)}, bf16[48,96,128]{2,1,0:T(8,128)(2,1)}, u32[]{:S(2)}, u32[]{:S(2)}) collective-permute-start(bf16[48,96,128]{2,1,0:T(8,128)(2,1)} %triangle.14.refs_12_), channel_id=1, source_target_pairs={{0,6},{1,3},{2,0},{3,5},{4,2},{5,7},{6,4},{7,1},{8,14},{9,11},{10,... | collective-permute-start | bytes 3538952 | tf_op jit(solution)/shard_map/ppermute | solution.py:290
where the time goes:
time: 425 us; the launch traced here: 423 us
  Pallas kernels  274 us (64%)
  waiting for transfers between devices  83 us (20%)
  starting transfers between devices  28.9 us (7%)
  local copies, waits for them, and re-layouts  23.5 us (6%)
  other arithmetic  12.8 us (3%)
    pallas_call x12, Pallas kernels, project(): pl.pallas_call(functools.partial(proj_kernel, sides, [g for _, _, g in pi...  135 us
    pallas_call x8, Pallas kernels, triangle(): pl.pallas_call(functools.partial(tri_kernel, nb, cb, widths, cut, len(dep...  133 us
    ppermute x33, waiting for transfers between devices, send(): return lax.ppermute(x, 'dap', perm)  83 us
    ppermute x33, starting transfers between devices, send(): return lax.ppermute(x, 'dap', perm)  28.9 us
  transfers between devices with their start and end apart: 33, of which 8 were waited for; matrix products, arithmetic and copies ran while one was open for 6% of the time, Pallas kernels for 55%

commit v1 on v0

v1 whole, which is shorter than its diff:
```python
import functools

import jax
import jax.numpy as jnp
from jax import lax
from jax.experimental import pallas as pl
from jax.experimental.pallas import tpu as pltpu
from jax.sharding import PartitionSpec as P


LN_EPS = 1e-5
F32 = jnp.float32
BF = jnp.bfloat16
RB = 16
LANES = 128
VMEM = 67043328
ROWS_AT_ONCE = 8
PAIRS = 4
ANY = pl.BlockSpec(memory_space=pl.ANY)


def norm_columns(x, scale, bias):
    inv = 1.0 / x.shape[0]
    cen = x - jnp.sum(x, axis=0, keepdims=True) * inv
    var = jnp.sum(cen * cen, axis=0, keepdims=True) * inv
    return (cen * lax.rsqrt(var + LN_EPS) * scale + bias).astype(BF)


def fill(dst, piece_refs, pos_ref, segments):
    at = 0
    for ref, lengths in zip(piece_refs, segments):
        start = 0
        for length in lengths:
            dst[:, pl.ds(pl.multiple_of(pos_ref[at], RB), length), :] = ref[:, start:start + length, :]
            start += length
            at += 1
    return at


def proj_kernel(sides, segments, chosen, z_out, extra, pos_ref, *refs):
    pieces = len(segments)
    z_refs, refs = refs[:pieces], refs[pieces:]
    m_ref, s_ref, b_ref, w_ref = refs[:4]
    refs = refs[4 + extra:]
    outs, refs = refs[:sides], refs[sides:]
    keep = sides == 2
    if keep:
        zn_out, refs = refs[0], refs[1:]
    if z_out:
        zkept, refs = refs[0], refs[1:]
    znm, tmp = refs[:2]
    refs = refs[2:]
    rows, n, d = z_refs[0].shape[0], m_ref.shape[1], z_refs[0].shape[2]
    ka = znm.shape[1]
    zfull = z_refs[0]
    at = len(segments[0])
    if pieces > 1:
        zfull, refs = (zkept, refs) if z_out and chosen is None else (refs[0], refs[1:])
        at = fill(zfull, z_refs, pos_ref, segments)
    zn_ref = None
    if keep:
        zn_ref = zn_out if chosen is None else refs[0]
    ones_row = lax.broadcasted_iota(jnp.int32, (ka - d, LANES), 0) == 0
    unroll = 4

    @pl.loop(0, rows, step=unroll)
    def _(i0):
        for u in range(unroll):
            i = i0 + u
            pair = i0 // 2 + u // 2
            m = m_ref[pl.ds(i, 1), :]
            for t in range(n // LANES):
                sl = slice(t * LANES, (t + 1) * LANES)
                wide = slice((u % 2) * n + t * LANES, (u % 2) * n + (t + 1) * LANES)
                y = norm_columns(zfull[i, sl, :].T.astype(F32), s_ref[...], b_ref[...])
                if keep:
                    zn_ref[i, sl, :] = y.T
                znm[pair, :d, wide] = y * m[:, sl].astype(BF)
                znm[pair, d:, wide] = jnp.where(ones_row, jnp.broadcast_to(m[:, sl], ones_row.shape), 0.0).astype(BF)

    parts, half = w_ref.shape[1], w_ref.shape[2] // 2

    @pl.loop(0, rows // 2, unroll=PAIRS)
    def _(i):
        rhs = znm[i]
        for sd in range(sides):
            for h in range(parts):
                p = jnp.dot(w_ref[sd, h], rhs, preferred_element_type=F32)
                act = ((jnp.tanh(p[half:]) + 1.0) * p[:half]).astype(BF)
                for e in range(2):
                    tmp[sd, 2 * i + e, h * half:(h + 1) * half, :] = act[:, e * n:(e + 1) * n]

    @pl.loop(0, parts * half // RB, unroll=2)
    def _(k):
        k0 = pl.multiple_of(k * RB, RB)
        for sd in range(sides):
            outs[sd][pl.ds(k0, RB)] = jnp.transpose(tmp[sd, :, pl.ds(k0, RB), :], (1, 0, 2))

    if chosen is not None:
        start = 0
        for length in chosen:
            place = pl.ds(pl.multiple_of(pos_ref[at], RB), length)
            zn_out[:, start:start + length, :] = zn_ref[:, place, :]
            zkept[:, start:start + length, :] = zfull[:, place, :]
            start += length
            at += 1


def project(pieces, pos, mask, params, layer, sides, r0, r, total, chosen=None, z_out=False, keep=None, deps=()):
    scale, bias, w = params
    n = mask.shape[1]
    d = pieces[0][0].shape[2]
    parts, half2, ka = w.shape[2:]
    c = parts * half2 // 2
    blk = r0 // RB
    full = sides == 2
    b_shape, b_spec = jax.ShapeDtypeStruct((c, r, n), BF), pl.BlockSpec((c, RB, n), lambda i, pos: (0, i, 0))
    out_shape, out_specs = [b_shape], [b_spec]
    width = n if chosen is None else sum(chosen)
    if full:
        kept = 2 if z_out else 1
        out_shape = [jax.ShapeDtypeStruct((c, total, n), BF), b_shape] + [jax.ShapeDtypeStruct((total, width, d), BF)] * kept
        out_specs = [pl.BlockSpec((c, RB, n), lambda i, pos: (0, i + blk, 0)), b_spec] + [pl.BlockSpec((RB, width, d), lambda i, pos: (i + blk, 0, 0))] * kept
    scratch = [pltpu.VMEM((RB // 2, ka, 2 * n), BF), pltpu.VMEM((sides, RB, c, n), BF)]
    count = len(pieces)
    if count > 1 and not (z_out and chosen is None):
        scratch = scratch + [pltpu.VMEM((RB, n, d), BF)]
    if chosen is not None:
        scratch = scratch + [pltpu.VMEM((RB, n, d), BF)]
    keep = tuple(keep or ())
    extra = keep + tuple(deps)
    spec = pltpu.PrefetchScalarGridSpec(
        num_scalar_prefetch=1,
        grid=(r // RB,),
        in_specs=[pl.BlockSpec((RB, x.shape[1], d), functools.partial(lambda f, i, pos: (i + f, 0, 0), f // RB)) for x, f, _ in pieces]
        + [
            pl.BlockSpec((RB, n), lambda i, pos: (i + blk, 0)),
            pl.BlockSpec((None, d, LANES), lambda i, pos: (layer, 0, 0)),
            pl.BlockSpec((None, d, LANES), lambda i, pos: (layer, 0, 0)),
            pl.BlockSpec((None, sides) + w.shape[2:], lambda i, pos: (layer, 2 - sides, 0, 0, 0)),
        ]
        + [ANY] * len(extra),
        out_specs=out_specs,
        scratch_shapes=scratch,
    )
    first = 1 + count + 4
    return pl.pallas_call(
        functools.partial(proj_kernel, sides, [g for _, _, g in pieces], chosen, z_out, len(extra)),
        grid_spec=spec,
        out_shape=out_shape,
        name="project",
        input_output_aliases={first: 0, first + 1: 2, first + 2: 3} if keep else {},
        cost_estimate=pl.CostEstimate(flops=16 * sides * r * n * d * c, bytes_accessed=2 * r * n * d * (2 + sides), transcendentals=0),
        compiler_params=pltpu.CompilerParams(vmem_limit_bytes=VMEM),
    )(pos, *[x for x, _, _ in pieces], mask, scale, bias, w, *extra)


def tri_kernel(nb, cb, widths, spread, extra, pos_ref, a_ref, *refs):
    count = len(widths)
    b_refs, z_refs, zn_refs, refs = refs[:count], refs[count:2 * count], refs[2 * count:3 * count], refs[3 * count:]
    ls_ref, lb_ref, wo_ref, bo_ref, wg_ref, bg_ref = refs[:6]
    o_ref, acc, on = refs[6 + extra:]
    step = pl.program_id(0)
    c = acc.shape[0]
    width = sum(widths)

    @pl.when(step < nb)
    def _():
        @pl.loop(0, cb, step=RB)
        def _(k0):
            for k in range(RB):
                both = jnp.concatenate([b[k0 + k] for b in b_refs], axis=0)
                acc[step * cb + k0 + k] = lax.dot_general(a_ref[k0 + k], both, (((1,), (1,)), ((), ())), preferred_element_type=F32)

    @pl.when(step >= nb)
    def _():
        ib = pl.multiple_of((step - nb) * RB, RB)
        zero = jnp.zeros((RB, width), F32)

        def block(k):
            return acc[pl.ds(pl.multiple_of(k * RB, RB), RB), pl.ds(ib, RB), :]

        mean = lax.fori_loop(0, c // RB, lambda k, t: t + jnp.sum(block(k), axis=0), zero) * (1.0 / c)

        def squares(k, t):
            v = block(k) - mean[None]
            return t + jnp.sum(v * v, axis=0)

        rstd = lax.rsqrt(lax.fori_loop(0, c // RB, squares, zero) * (1.0 / c) + LN_EPS)

        @pl.loop(0, c // RB)
        def _(k):
            k0 = pl.multiple_of(k * RB, RB)
            for t in range(0, width, LANES):
                sl = slice(t, min(t + LANES, width))
                v = acc[pl.ds(k0, RB), pl.ds(ib, RB), sl]
                lanes = sl.stop - sl.start
                v = (v - mean[None, :, sl]) * rstd[None, :, sl] * ls_ref[pl.ds(k0, RB), :, :lanes] + lb_ref[pl.ds(k0, RB), :, :lanes]
                on[:, pl.ds(k0, RB), sl] = jnp.transpose(v.astype(BF), (1, 0, 2))

        g_rows = ROWS_AT_ONCE

        @pl.loop(0, RB, step=g_rows)
        def _(i0):
            rs = pl.ds(i0, g_rows)
            start = 0
            for h, wd in enumerate(widths):
                ont = jnp.transpose(on[rs, :, start:start + wd], (0, 2, 1)).reshape(g_rows * wd, c)
                u = jnp.dot(ont, wo_ref[...], preferred_element_type=F32) + bo_ref[...]
                u = u.astype(BF).astype(F32)
                g = jnp.dot(zn_refs[h][rs].reshape(g_rows * wd, -1), wg_ref[...], preferred_element_type=F32) + bg_ref[...]
                new = z_refs[h][rs].astype(F32) + (jax.nn.sigmoid(g) * u).reshape(g_rows, wd, -1)
                at = pl.ds(pl.multiple_of(pos_ref[h], RB), wd) if spread else slice(start, start + wd)
                o_ref[rs, at, :] = new.astype(BF)
                start += wd


def triangle(pos, a, bs, z, zn, tail, layer, out_width=None, deps=()):
    c, r, n = a.shape
    d = z.shape[2]
    cb = 2 * RB
    nb = c // cb
    widths = [b.shape[1] for b in bs]
    width = sum(widths)

    def first(s, pos):
        return jnp.minimum(s, nb - 1), 0, 0

    def later(s):
        return jnp.maximum(s - nb, 0)

    def of_layer(x):
        return pl.BlockSpec((None,) + x.shape[1:], lambda s, pos: (layer,) + (0,) * (x.ndim - 1))

    def columns(h):
        return pl.BlockSpec((pl.Element(RB), pl.Element(widths[h]), pl.Element(d)), lambda s, pos: (later(s) * RB, pl.multiple_of(pos[h], RB), 0))

    wide = out_width or width
    spec = pltpu.PrefetchScalarGridSpec(
        num_scalar_prefetch=1,
        grid=(nb + r // RB,),
        in_specs=[pl.BlockSpec((cb, r, n), first)]
        + [pl.BlockSpec((cb, j, n), first) for j in widths]
        + [columns(h) for h in range(len(widths))] * 2
        + [of_layer(x) for x in tail]
        + [ANY] * len(deps),
        out_specs=pl.BlockSpec((RB, wide, d), lambda s, pos: (later(s), 0, 0)),
        scratch_shapes=[pltpu.VMEM((c, r, width), F32), pltpu.VMEM((RB, c, width), BF)],
    )
    return pl.pallas_call(
        functools.partial(tri_kernel, nb, cb, widths, out_width is not None, len(deps)),
        grid_spec=spec,
        out_shape=jax.ShapeDtypeStruct((r, wide, d), BF),
        name="triangle",
        cost_estimate=pl.CostEstimate(flops=16 * r * n * width * c, bytes_accessed=2 * c * n * (r + width), transcendentals=0),
        compiler_params=pltpu.CompilerParams(vmem_limit_bytes=VMEM),
    )(pos, a, *bs, *[z] * len(widths), *[zn] * len(widths), *tail, *deps)


def patch_kernel(pos_ref, piece_ref, whole_ref, out_ref):
    half = piece_ref.shape[1] // 2
    for h in range(2):
        out_ref[:, pl.ds(pl.multiple_of(pos_ref[1 + h], RB), half), :] = piece_ref[:, h * half:(h + 1) * half, :]


def patch(whole, piece, pos):
    r, j, d = piece.shape
    spec = pltpu.PrefetchScalarGridSpec(
        num_scalar_prefetch=1,
        grid=(r // RB,),
        in_specs=[pl.BlockSpec((RB, j, d), lambda i, pos: (i, 0, 0)), ANY],
        out_specs=pl.BlockSpec((RB, j, d), lambda i, pos: (i, pos[0], 0)),
    )
    return pl.pallas_call(
        patch_kernel,
        grid_spec=spec,
        out_shape=jax.ShapeDtypeStruct(whole.shape, BF),
        name="patch",
        input_output_aliases={2: 0},
    )(pos, piece, whole)


def side_weights(w_in, b_in):
    layers, d, c4 = w_in.shape
    w = jnp.transpose(w_in, (0, 2, 1))
    w = jnp.concatenate([w, b_in[:, :, None], jnp.zeros((layers, c4, 15), w_in.dtype)], axis=2) * 0.5
    w = w.reshape(layers, 2, 2, 2, c4 // 8, d + 16)
    return jnp.transpose(w, (0, 1, 3, 2, 4, 5)).reshape(layers, 2, 2, c4 // 4, d + 16)


def solution(mesh):
    row_spec = P(('batch', 'dap'), None, None)
    mask_spec = P(('batch', 'dap'), None)
    vec_spec = P(None, None)
    mat_spec = P(None, None, None)
    size = mesh.shape['dap']
    chips = size // 2
    side = [1 - 2 * (i % 2) for i in range(size)]
    to_helper = [(i, (i + 2 * side[i]) % size) for i in range(size)]
    to_other = [(i, (i - 2 * side[i]) % size) for i in range(size)]
    to_partner = [(i, i ^ 1) for i in range(size)]

    def device_fn(z_rows, mask_rows, ln_in_scale, ln_in_bias, w_in, b_in, w_gate, b_gate, ln_out_scale, ln_out_bias, w_out, b_out):
        def send(x, perm):
            return lax.ppermute(x, 'dap', perm)

        layers, d, _ = w_in.shape
        rows, n, _ = z_rows.shape
        lo = RB
        hi = rows - lo
        parts = ((0, hi), (hi, lo))
        index = lax.axis_index('dap')
        core, chip = index % 2, index // 2
        sgn = 1 - 2 * core

        def columns(segs, shift=0):
            at = [2 * rows * lax.rem(chip + (k + shift) * sgn + 4 * chips, chips) + rows * jnp.where(flip, 1 - core, core) + r0 for k, flip, r0, _ in segs]
            return jnp.stack(at).astype(jnp.int32)

        def lengths(segs):
            return [g[3] for g in segs]

        def whole(k):
            return [(k, flip, 0, rows) for flip in (0, 1)]

        mid = [[(k, flip, r0, r) for k in (1, -1) for flip in (0, 1)] for r0, r in parts]
        far_split = [(2, flip, r0, r) for r0, r in parts for flip in (0, 1)]

        z_hi = z_rows[:hi]
        near_in, other_in = [send(z_hi, to_helper)], [send(z_hi, to_other)]
        z_lo = z_rows[hi:]
        near_in.append(send(z_lo, to_helper))
        other_in.append(send(z_lo, to_other))
        mask = mask_rows.astype(F32)
        mask_near, mask_other = send(mask, to_helper), send(mask, to_other)

        scale = jnp.broadcast_to(ln_in_scale.astype(F32)[:, :, None], (layers, d, LANES))
        bias = jnp.broadcast_to(ln_in_bias.astype(F32)[:, :, None], (layers, d, LANES))
        params = (scale, bias, side_weights(w_in, b_in))
        c = ln_out_scale.shape[1]
        ls = jnp.broadcast_to(ln_out_scale.astype(F32)[:, :, None, None], (layers, c, 1, LANES))
        lb = jnp.broadcast_to(ln_out_bias.astype(F32)[:, :, None, None], (layers, c, 1, LANES))
        tail = (ls, lb, w_out, b_out.astype(F32)[:, None], w_gate, b_gate.astype(F32)[:, None])

        start = jnp.zeros((1,), jnp.int32)
        own_p, near_p, other_p, pos = None, None, None, None

        for layer in range(layers):
            final = layer + 1 == layers
            if layer == 0:
                far_segs = far_split
                a, b, zn = project([(z_rows, 0, [n])], start, mask, params, layer, 2, 0, rows, rows)
                b_p = send(b, to_partner)
                z_own = z_rows
                p0 = triangle(columns(whole(0)), a, [b, b_p], z_own, zn, tail, layer, None, (b,))
                p0_near, p0_other = send(p0, to_helper), send(p0, to_other)
                last = (p0,)
                near = None
                bn, bn_p, bo, bo_p = [None] * 2, [None] * 2, [None] * 2, [None] * 2
                for q, (r0, r) in enumerate(parts):
                    where = jnp.concatenate([start, columns(far_segs, -1)])
                    a_n, bn[q], zn_n, z_n = project([(near_in[q], 0, [n])], where, mask_near, params, layer, 2, r0, r, rows, lengths(far_segs), True, near, last)
                    near = (a_n, zn_n, z_n)
                    bn_p[q] = send(bn[q], to_partner)
                    bo[q], = project([(other_in[q], 0, [n])], start, mask_other, params, layer, 1, r0, r, rows, None, False, None, (bn[q],))
                    last = (bo[q],)
                    bo_p[q] = send(bo[q], to_partner)
                    if q == 0:
                        c1 = triangle(columns(mid[0]), a, [bo[0], bn_p[0], bn[0], bo_p[0]], z_own, zn, tail, layer, None, last)
                        last = (c1,)
                        c1_near, c1_other = send(c1, to_helper), send(c1, to_other)
                far_b = [bo[0], bn_p[0], bo[1], bn_p[1]]
            else:
                far_segs = whole(2)
                a, b, zn, z_own = project(own_p, pos[0], mask, params, layer, 2, 0, rows, rows, None, True, None, last)
                b_p = send(b, to_partner)
                where = jnp.concatenate([pos[1], columns(far_segs, -1)])
                a_n, bn, zn_n, z_n = project(near_p, where, mask_near, params, layer, 2, 0, rows, rows, lengths(far_segs), True, None, (b,))
                near = (a_n, zn_n, z_n)
                bn_p = send(bn, to_partner)
                bo, = project(other_p, pos[2], mask_other, params, layer, 1, 0, rows, rows, None, False, None, (bn,))
                bo_p = send(bo, to_partner)
                last = (bo,)
                far_b = [bo, bn_p]
            at, ends = 0, []
            for x in far_b:
                ends.append(at)
                at += x.shape[1]
            far = triangle(jnp.array(ends, jnp.int32), near[0], far_b, near[2], near[1], tail, layer, None, last)
            last = (far,)
            p3 = send(far, to_other)
            if layer == 0:
                c2 = triangle(columns(mid[1]), a, [bo[1], bn_p[1], bn[1], bo_p[1]], z_own, zn, tail, layer, None, last)
                last = (c2,)
                pieces = [(p0, whole(0)), (c1, mid[0]), (c2, mid[1])]
                near_got, other_got = [p0_near, c1_near, send(c2, to_helper)], [p0_other, c1_other, send(c2, to_other)]
            else:
                segs = whole(0) + whole(1) + whole(-1)
                rest = triangle(columns(segs), a, [b, b_p, bo, bn_p, bn, bo_p], z_own, zn, tail, layer, n if final else None, last)
                last = (rest,)
                if final:
                    block = lax.rem(chip + 2, chips)
                    return patch(rest, p3, jnp.stack([block, core * rows, (1 - core) * rows]).astype(jnp.int32))
                pieces = [(rest, segs)]
                near_got, other_got = [send(rest, to_helper)], [send(rest, to_other)]
            pieces.append((p3, far_segs))
            near_got.append(far)
            other_got.append(send(p3, to_other))
            every = [g for _, segs in pieces for g in segs]
            own_p = [(x, 0, lengths(segs)) for x, segs in pieces]
            near_p = [(x, 0, lengths(segs)) for x, (_, segs) in zip(near_got, pieces)]
            other_p = [(x, 0, lengths(segs)) for x, (_, segs) in zip(other_got, pieces)]
            pos = [columns(every), columns(every, -1), columns(every, 1)]

    return jax.shard_map(device_fn, mesh=mesh, in_specs=(row_spec, mask_spec, vec_spec, vec_spec, mat_spec, vec_spec, mat_spec, vec_spec, vec_spec, vec_spec, mat_spec, vec_spec), out_specs=row_spec, check_vma=False)
```

time: 425 us -> 360 us (0.85)
  Pallas kernels: 274 us -> 222 us
  waiting for transfers between devices: 83 us -> 91.1 us
  other arithmetic: 12.8 us -> 5.9 us
  local copies, waits for them, and re-layouts: 23.5 us -> 17 us
  starting transfers between devices: 28.9 us -> 22.4 us
    pallas_call x12 -> x8, Pallas kernels: 135 us -> 108 us  [project(): pl.pallas_call(functools.partial(proj_kernel, sides, [g for _, _, g in pi...]
    pallas_call x9 -> x7, Pallas kernels: 139 us -> 114 us  [the longest x6 111 us: triangle(): pl.pallas_call(functools.partial(tri_kernel, nb, cb, widths, out_width is...]
    ppermute x33 -> x23, waiting for transfers between devices: 83 us -> 91.1 us  [send(): return lax.ppermute(x, 'dap', perm)]
    ppermute x33 -> x23, starting transfers between devices: 28.9 us -> 22.4 us  [send(): return lax.ppermute(x, 'dap', perm)]
    convert_element_type x5 -> x0, other arithmetic: 6.33 us -> none  [the longest x1 1.3 us: device_fn(): ln_out_scale[layer].astype(F32)[:, None, None]]
    broadcast_in_dim x8 -> x5, local copies, waits for them, and re-layouts: 8.63 us -> 4.12 us  [the longest x1 1.4 us: device_fn(): jnp.broadcast_to(ln_in_scale.astype(F32)[:, :, None], (layers, d, LANES))]
  transfers between devices with their start and end apart: 33 -> 23, of which waited for: 8 -> 6; matrix products, arithmetic and copies ran while one was open for 6% -> 4% of each run, Pallas kernels for 55% -> 53%
where the time goes in v1:
time: 360 us; the launch traced here: 359 us
  Pallas kernels  222 us (62%)
  waiting for transfers between devices  91.1 us (25%)
  starting transfers between devices  22.4 us (6%)
  local copies, waits for them, and re-layouts  17 us (5%)
  other arithmetic  5.9 us (2%)
    pallas_call x6, Pallas kernels, triangle(): pl.pallas_call(functools.partial(tri_kernel, nb, cb, widths, out_width is...  111 us
    pallas_call x8, Pallas kernels, project(): pl.pallas_call(functools.partial(proj_kernel, sides, [g for _, _, g in pi...  108 us
    ppermute x23, waiting for transfers between devices, send(): return lax.ppermute(x, 'dap', perm)  91.1 us
    ppermute x23, starting transfers between devices, send(): return lax.ppermute(x, 'dap', perm)  22.4 us
  transfers between devices with their start and end apart: 23, of which 6 were waited for; matrix products, arithmetic and copies ran while one was open for 4% of the time, Pallas kernels for 53%

profile of v1, /device:TPU:113, one launch (start us, length us, event | category | flops | bytes accessed | tf_op | source)
XLA Modules:
  0.0 358.8 jit_solution(10459239110502421890)
XLA Ops:
  0.0 1.1 copy.23
  1.1 1.1 concatenate.20
  2.3 0.1 pad.10.clone
  2.3 0.1 fusion
  2.5 0.9 copy.25
  3.4 1.5 convert_element_type.17.refs_1_.refs_4_
  4.9 1.4 broadcast_in_dim.18.refs_2_.refs_5_
  6.3 0.7 broadcast_in_dim.19.refs_3_.refs_6_
  7.0 17.7 %project.8 = (bf16[128,48,384]{2,1,0:T(8,128)(2,1)}, bf16[128,48,384]{2,1,0:T(8,128)(2,1)}, bf16[48,384,128]{2,1,0:T(8,128)(2,1)}) custom-call(s32[1]{0:T(128)} %constant.137.clone.1.pos_ref, bf16[48,384,128]{2,1,0:T(8,128)(2,1)} %refs_7_.3, f32[48,384]{1,0:T(8,128)} %convert_element_type.17.refs_1_.refs_4_, ...), custom_call_target="tpu_custom_call" | custom-call | flops 9663676416 | bytes 18874368 | tf_op jit(solution)/shard_map/project/pallas_call | solution.py:147
  24.8 0.0 copy-start.1
  24.8 0.0 copy-start.2
  24.8 0.8 collective-permute-start
  25.6 3.8 %slice.6 = bf16[32,384,128]{2,1,0:T(8,128)(2,1)} slice(bf16[48,384,128]{2,1,0:T(8,128)(2,1)} %refs_7_.3), slice={[0:32], [0:384], [0:128]} | slice | bytes 6291456 | tf_op jit(solution)/shard_map/slice | solution.py:329
  29.4 3.6 %collective-permute-start.4 = (bf16[32,384,128]{2,1,0:T(8,128)(2,1)}, bf16[32,384,128]{2,1,0:T(8,128)(2,1)}, u32[]{:S(2)}, u32[]{:S(2)}) collective-permute-start(bf16[32,384,128]{2,1,0:T(8,128)(2,1)} %slice.6), channel_id=1, source_target_pairs={{0,2},{1,7},{2,4},{3,1},{4,6},{5,3},{6,0},{7,5},{8,10},{9,15},{10,... | collective-permute-start | bytes 9437192 | tf_op jit(solution)/shard_map/ppermute | solution.py:305
  33.0 2.7 collective-permute-start.5
  35.7 0.0 collective-permute-start.3
  35.7 0.6 broadcast_in_dim.47
  36.3 0.6 broadcast_in_dim.48
  36.9 0.6 concatenate.19.pos_ref
  37.5 0.6 pad_add_fusion.1.pos_ref
  38.1 0.0 collective-permute-done.refs_1_
  38.1 1.0 broadcast_in_dim.41.refs_6_.refs_12_.refs_18_
  39.1 1.0 broadcast_in_dim.42.refs_7_.refs_13_.refs_19_
  40.1 14.6 %triangle.6.refs_5_.refs_0_ = bf16[48,96,128]{2,1,0:T(8,128)(2,1)} custom-call(s32[2]{0:T(128)} %pad_add_fusion.1.pos_ref, bf16[128,48,384]{2,1,0:T(8,128)(2,1)} %get-tuple-element.24.a_ref, bf16[128,48,384]{2,1,0:T(8,128)(2,1)} %get-tuple-element.25.refs_0_.refs_12_, bf16[128,48,384]{2,1,0:T(8,128)(2,1)} %collective-permute-done.refs_1_, ...), custom_call_target="tpu_custom_call" | custom-call | flops 3623878656 | bytes 14155776 | tf_op jit(solution)/shard_map/triangle/pallas_call | solution.py:250
  54.7 47.7 %collective-permute-done.5.refs_1_.refs_4_ = f32[48,384]{1,0:T(8,128)} collective-permute-done((f32[48,384]{1,0:T(8,128)}, f32[48,384]{1,0:T(8,128)}, u32[]{:S(2)}, u32[]{:S(2)}) %collective-permute-start.5) | collective-permute-done | bytes 73760 | tf_op jit(solution)/shard_map/ppermute | solution.py:305
  102.4 13.7 %project.9 = (bf16[128,48,384]{2,1,0:T(8,128)(2,1)}, bf16[128,32,384]{2,1,0:T(8,128)(2,1)}, bf16[48,96,128]{2,1,0:T(8,128)(2,1)}, bf16[48,96,128]{2,1,0:T(8,128)(2,1)}) custom-call(s32[5]{0:T(128)} %concatenate.19.pos_ref, bf16[32,384,128]{2,1,0:T(8,128)(2,1)} %collective-permute-done.4.refs_0_, f32[48,384]{1,0:T(8,128)} %collective-permute-done.5.refs_1_.refs_4_, ...), custom_call_target="tpu_custom_call" | custom-call | flops 6442450944 | bytes 12582912 | tf_op jit(solution)/shard_map/project/pallas_call | solution.py:147
  116.1 9.2 %project.10.refs_0_.refs_18_ = bf16[128,32,384]{2,1,0:T(8,128)(2,1)} custom-call(s32[1]{0:T(128)} %constant.137.clone.1.pos_ref, bf16[32,384,128]{2,1,0:T(8,128)(2,1)} %collective-permute-done.2.refs_0_, f32[48,384]{1,0:T(8,128)} %collective-permute-done.3.refs_1_.refs_4_, f32[2,128,128]{2,1,0:T(8,128)} %broadcast_in_dim.18.refs_2_.refs_5_, ...), custom_call_target="tpu_custom_call" | custom-call | flops 3221225472 | bytes 9437184 | tf_op jit(solution)/shard_map/project/pallas_call | solution.py:147
  125.2 0.5 collective-permute-start.6
  125.7 2.7 slice.7
  128.4 3.4 collective-permute-start.10
  131.9 0.6 pad_add_fusion.2.pos_ref
  132.5 3.3 collective-permute-done.6.refs_1_
  135.7 18.5 %triangle.7.refs_8_.refs_1_ = bf16[48,128,128]{2,1,0:T(8,128)(2,1)} custom-call(s32[4]{0:T(128)} %pad_add_fusion.2.pos_ref, bf16[128,48,384]{2,1,0:T(8,128)(2,1)} %get-tuple-element.24.a_ref, bf16[128,32,384]{2,1,0:T(8,128)(2,1)} %project.10.refs_0_.refs_18_, bf16[128,32,384]{2,1,0:T(8,128)(2,1)} %collective-permute-done.6.refs_1_, ...), custom_call_target="tpu_custom_call" | custom-call | flops 4831838208 | bytes 17301504 | tf_op jit(solution)/shard_map/triangle/pallas_call | solution.py:250
  154.2 11.6 %collective-permute-done.10.refs_0_ = bf16[16,384,128]{2,1,0:T(8,128)(2,1)} collective-permute-done((bf16[16,384,128]{2,1,0:T(8,128)(2,1)}, bf16[16,384,128]{2,1,0:T(8,128)(2,1)}, u32[]{:S(2)}, u32[]{:S(2)}) %collective-permute-start.10) | collective-permute-done | bytes 1572896 | tf_op jit(solution)/shard_map/ppermute | solution.py:305
  165.8 8.8 %project.11 = (bf16[128,48,384]{2,1,0:T(8,128)(2,1)}, bf16[128,16,384]{2,1,0:T(8,128)(2,1)}, bf16[48,96,128]{2,1,0:T(8,128)(2,1)}, bf16[48,96,128]{2,1,0:T(8,128)(2,1)}) custom-call(s32[5]{0:T(128)} %concatenate.19.pos_ref, bf16[16,384,128]{2,1,0:T(8,128)(2,1)} %collective-permute-done.10.refs_0_, ...), custom_call_target="tpu_custom_call", output_to_operand_aliasing={{0}: (6, {}), {2}: (7, {}), {3}: (8, {})} | custom-call | flops 3221225472 | bytes 6291456 | tf_op jit(solution)/shard_map/project/pallas_call | solution.py:147
  174.7 5.9 %project.12.refs_2_.refs_18_.refs_0_ = bf16[128,16,384]{2,1,0:T(8,128)(2,1)} custom-call(s32[1]{0:T(128)} %constant.137.clone.1.pos_ref, bf16[16,384,128]{2,1,0:T(8,128)(2,1)} %collective-permute-done.9.refs_0_, f32[48,384]{1,0:T(8,128)} %collective-permute-done.3.refs_1_.refs_4_, f32[2,128,128]{2,1,0:T(8,128)} %broadcast_in_dim.18.refs_2_.refs_5_, ...), custom_call_target="tpu_custom_call" | custom-call | flops 1610612736 | bytes 4718592 | tf_op jit(solution)/shard_map/project/pallas_call | solution.py:147
  180.6 0.5 collective-permute-start.12
  181.1 3.4 collective-permute-start.1
  184.5 17.1 %triangle.8.refs_18_.refs_3_ = bf16[48,96,128]{2,1,0:T(8,128)(2,1)} custom-call(s32[4]{0:T(128)} %constant.140.clone.pos_ref, bf16[128,48,384]{2,1,0:T(8,128)(2,1)} %get-tuple-element.32.a_ref, bf16[128,32,384]{2,1,0:T(8,128)(2,1)} %project.10.refs_0_.refs_18_, bf16[128,32,384]{2,1,0:T(8,128)(2,1)} %collective-permute-done.6.refs_1_, ...), custom_call_target="tpu_custom_call" | custom-call | flops 3623878656 | bytes 14155776 | tf_op jit(solution)/shard_map/triangle/pallas_call | solution.py:250
  201.6 0.1 collective-permute-start.14
  201.8 2.6 collective-permute-start.8
  204.4 0.6 stack.173.pos_ref
  205.0 0.6 concatenate.15.pos_ref
  205.7 0.6 pad_add_fusion.3.pos_ref
  206.3 0.0 collective-permute-start.16
  206.3 15.2 %triangle.9.refs_2_.refs_8_ = bf16[48,64,128]{2,1,0:T(8,128)(2,1)} custom-call(s32[4]{0:T(128)} %pad_add_fusion.3.pos_ref, bf16[128,48,384]{2,1,0:T(8,128)(2,1)} %get-tuple-element.24.a_ref, bf16[128,16,384]{2,1,0:T(8,128)(2,1)} %project.12.refs_2_.refs_18_.refs_0_, bf16[128,16,384]{2,1,0:T(8,128)(2,1)} %collective-permute-done.11.refs_3_.refs_1_, ...), custom_call_target="tpu_custom_call" | custom-call | flops 2415919104 | bytes 11010048 | tf_op jit(solution)/shard_map/triangle/pallas_call | solution.py:250
  221.6 2.7 collective-permute-start.13
  224.3 6.2 %collective-permute-done.14.refs_3_ = bf16[48,96,128]{2,1,0:T(8,128)(2,1)} collective-permute-done((bf16[48,96,128]{2,1,0:T(8,128)(2,1)}, bf16[48,96,128]{2,1,0:T(8,128)(2,1)}, u32[]{:S(2)}, u32[]{:S(2)}) %collective-permute-start.14) | collective-permute-done | bytes 1179680 | tf_op jit(solution)/shard_map/ppermute | solution.py:305
  230.5 19.7 %project.13 = (bf16[128,48,384]{2,1,0:T(8,128)(2,1)}, bf16[128,48,384]{2,1,0:T(8,128)(2,1)}, bf16[48,384,128]{2,1,0:T(8,128)(2,1)}, bf16[48,384,128]{2,1,0:T(8,128)(2,1)}) custom-call(s32[14]{0:T(128)} %stack.173.pos_ref, bf16[48,96,128]{2,1,0:T(8,128)(2,1)} %triangle.6.refs_5_.refs_0_, bf16[48,128,128]{2,1,0:T(8,128)(2,1)} %triangle.7.refs_8_.refs_1_, ...), custom_call_target="tpu_custom_call" | custom-call | flops 9663676416 | bytes 18874368 | tf_op jit(solution)/shard_map/project/pallas_call | solution.py:147
  250.2 0.1 collective-permute-start.17
  250.3 5.5 %collective-permute-done.13.refs_2_ = bf16[48,64,128]{2,1,0:T(8,128)(2,1)} collective-permute-done((bf16[48,64,128]{2,1,0:T(8,128)(2,1)}, bf16[48,64,128]{2,1,0:T(8,128)(2,1)}, u32[]{:S(2)}, u32[]{:S(2)}) %collective-permute-start.13) | collective-permute-done | bytes 786464 | tf_op jit(solution)/shard_map/ppermute | solution.py:305
  255.8 19.0 %project.14 = (bf16[128,48,384]{2,1,0:T(8,128)(2,1)}, bf16[128,48,384]{2,1,0:T(8,128)(2,1)}, bf16[48,96,128]{2,1,0:T(8,128)(2,1)}, bf16[48,96,128]{2,1,0:T(8,128)(2,1)}) custom-call(s32[16]{0:T(128)} %concatenate.15.pos_ref, bf16[48,96,128]{2,1,0:T(8,128)(2,1)} %collective-permute-done.1.refs_0_, bf16[48,128,128]{2,1,0:T(8,128)(2,1)} %collective-permute-done.8.refs_1_, ...), custom_call_target="tpu_custom_call" | custom-call | flops 9663676416 | bytes 18874368 | tf_op jit(solution)/shard_map/project/pallas_call | solution.py:147
  274.8 1.9 collective-permute-start.19
  276.6 0.6 stack.178.pos_ref
  277.3 0.1 collective-permute-start.21
  277.3 16.8 %collective-permute-done.17.refs_2_ = bf16[48,64,128]{2,1,0:T(8,128)(2,1)} collective-permute-done((bf16[48,64,128]{2,1,0:T(8,128)(2,1)}, bf16[48,64,128]{2,1,0:T(8,128)(2,1)}, u32[]{:S(2)}, u32[]{:S(2)}) %collective-permute-start.17) | collective-permute-done | bytes 786464 | tf_op jit(solution)/shard_map/ppermute | solution.py:305
  294.1 13.8 %project.15.refs_0_.refs_12_.refs_2_ = bf16[128,48,384]{2,1,0:T(8,128)(2,1)} custom-call(s32[14]{0:T(128)} %stack.178.pos_ref, bf16[48,96,128]{2,1,0:T(8,128)(2,1)} %collective-permute-done.15.refs_0_, bf16[48,128,128]{2,1,0:T(8,128)(2,1)} %collective-permute-done.16.refs_1_, bf16[48,64,128]{2,1,0:T(8,128)(2,1)} %collective-permute-done.17.refs_2_, ...), custom_call_target="tpu_custom_call" | custom-call | flops 4831838208 | bytes 14155776 | tf_op jit(solution)/shard_map/project/pallas_call | solution.py:147
  307.9 0.6 iota_multiply_fusion.pos_ref
  308.5 14.6 %triangle.10.refs_24_ = bf16[48,96,128]{2,1,0:T(8,128)(2,1)} custom-call(s32[2]{0:T(128)} %iota_multiply_fusion.pos_ref, bf16[128,48,384]{2,1,0:T(8,128)(2,1)} %get-tuple-element.36.a_ref, bf16[128,48,384]{2,1,0:T(8,128)(2,1)} %project.15.refs_0_.refs_12_.refs_2_, bf16[128,48,384]{2,1,0:T(8,128)(2,1)} %collective-permute-done.19.refs_1_.refs_3_, ...), custom_call_target="tpu_custom_call" | custom-call | flops 3623878656 | bytes 14155776 | tf_op jit(solution)/shard_map/triangle/pallas_call | solution.py:250
  323.1 0.0 collective-permute-start.20
  323.1 0.7 stack.179.pos_ref
  323.8 0.7 pad_add_fusion.pos_ref
  324.5 30.5 %triangle.11.whole_ref = bf16[48,384,128]{2,1,0:T(8,128)(2,1)} custom-call(s32[6]{0:T(128)} %stack.179.pos_ref, bf16[128,48,384]{2,1,0:T(8,128)(2,1)} %get-tuple-element.40.a_ref, bf16[128,48,384]{2,1,0:T(8,128)(2,1)} %get-tuple-element.35.refs_8_.refs_0_, bf16[128,48,384]{2,1,0:T(8,128)(2,1)} %collective-permute-done.21.refs_1_, ...), custom_call_target="tpu_custom_call" | custom-call | flops 10871635968 | bytes 33030144 | tf_op jit(solution)/shard_map/triangle/pallas_call | solution.py:250
  355.0 3.8 %patch.1 = bf16[48,384,128]{2,1,0:T(8,128)(2,1)} custom-call(s32[3]{0:T(128)} %pad_add_fusion.pos_ref, bf16[48,96,128]{2,1,0:T(8,128)(2,1)} %collective-permute-done.20.piece_ref, bf16[48,384,128]{2,1,0:T(8,128)(2,1)} %triangle.11.whole_ref), custom_call_target="tpu_custom_call", output_to_operand_aliasing={{}: (2, {})} | custom-call | tf_op jit(solution)/shard_map/patch/pallas_call | solution.py:274
  (32 shorter events, 0.1 us)
Async XLA Ops:
  0.0 6.3 %copy-start = (bf16[2,128]{1,0:T(2,128)(2,1)S(1)}, bf16[2,128]{1,0:T(2,128)(2,1)}, u32[]{:S(2)}) copy-start(bf16[2,128]{1,0:T(2,128)(2,1)} %param.17) | copy-start | bytes 1540
  24.8 10.9 %copy-start.3 = (bf16[2,128]{1,0:T(2,128)(2,1)S(1)}, bf16[2,128]{1,0:T(2,128)(2,1)}, u32[]{:S(2)}) copy-start(bf16[2,128]{1,0:T(2,128)(2,1)} %param.25) | copy-start | bytes 1540
  24.8 11.5 %copy-start.4 = (bf16[2,128]{1,0:T(2,128)(2,1)S(1)}, bf16[2,128]{1,0:T(2,128)(2,1)}, u32[]{:S(2)}) copy-start(bf16[2,128]{1,0:T(2,128)(2,1)} %param.21) | copy-start | bytes 1540
  24.8 13.3 %copy-start.1 = (bf16[2,128]{1,0:T(2,128)(2,1)S(1)}, bf16[2,128]{1,0:T(2,128)(2,1)}, u32[]{:S(2)}) copy-start(bf16[2,128]{1,0:T(2,128)(2,1)} %param.22) | copy-start | bytes 1540
  24.8 14.3 %copy-start.2 = (bf16[2,128]{1,0:T(2,128)(2,1)S(1)}, bf16[2,128]{1,0:T(2,128)(2,1)}, u32[]{:S(2)}) copy-start(bf16[2,128]{1,0:T(2,128)(2,1)} %param.23) | copy-start | bytes 1540
  24.8 13.3 %collective-permute-start = (bf16[128,48,384]{2,1,0:T(8,128)(2,1)}, bf16[128,48,384]{2,1,0:T(8,128)(2,1)}, u32[]{:S(2)}, u32[]{:S(2)}) collective-permute-start(bf16[128,48,384]{2,1,0:T(8,128)(2,1)} %get-tuple-element.25.refs_0_.refs_12_), channel_id=1, source_target_pairs={{0,1},{1,0},{2,3},{3,2},{4,5},{5,4},{6,7},{7,6},{8,9},{9,8},{10,11... | collective-permute-start | bytes 14155784 | tf_op jit(solution)/shard_map/ppermute | solution.py:305
  29.4 72.9 %collective-permute-start.4 = (bf16[32,384,128]{2,1,0:T(8,128)(2,1)}, bf16[32,384,128]{2,1,0:T(8,128)(2,1)}, u32[]{:S(2)}, u32[]{:S(2)}) collective-permute-start(bf16[32,384,128]{2,1,0:T(8,128)(2,1)} %slice.6), channel_id=1, source_target_pairs={{0,2},{1,7},{2,4},{3,1},{4,6},{5,3},{6,0},{7,5},{8,10},{9,15},{10,... | collective-permute-start | bytes 9437192 | tf_op jit(solution)/shard_map/ppermute | solution.py:305
  33.0 83.0 %collective-permute-start.2 = (bf16[32,384,128]{2,1,0:T(8,128)(2,1)}, bf16[32,384,128]{2,1,0:T(8,128)(2,1)}, u32[]{:S(2)}, u32[]{:S(2)}) collective-permute-start(bf16[32,384,128]{2,1,0:T(8,128)(2,1)} %slice.6), channel_id=1, source_target_pairs={{0,6},{1,3},{2,0},{3,5},{4,2},{5,7},{6,4},{7,1},{8,14},{9,11},{10,... | collective-permute-start | bytes 9437192 | tf_op jit(solution)/shard_map/ppermute | solution.py:305
  33.0 69.3 %collective-permute-start.5 = (f32[48,384]{1,0:T(8,128)}, f32[48,384]{1,0:T(8,128)}, u32[]{:S(2)}, u32[]{:S(2)}) collective-permute-start(f32[48,384]{1,0:T(8,128)} %convert_element_type.17.refs_1_.refs_4_), channel_id=1, source_target_pairs={{0,2},{1,7},{2,4},{3,1},{4,6},{5,3},{6,0},{7,5},{8,10},{9,15},{10,... | collective-permute-start | bytes 221192 | tf_op jit(solution)/shard_map/ppermute | solution.py:305
  35.7 80.3 %collective-permute-start.3 = (f32[48,384]{1,0:T(8,128)}, f32[48,384]{1,0:T(8,128)}, u32[]{:S(2)}, u32[]{:S(2)}) collective-permute-start(f32[48,384]{1,0:T(8,128)} %convert_element_type.17.refs_1_.refs_4_), channel_id=1, source_target_pairs={{0,6},{1,3},{2,0},{3,5},{4,2},{5,7},{6,4},{7,1},{8,14},{9,11},{10,... | collective-permute-start | bytes 221192 | tf_op jit(solution)/shard_map/ppermute | solution.py:305
  125.2 7.2 %collective-permute-start.7 = (bf16[128,32,384]{2,1,0:T(8,128)(2,1)}, bf16[128,32,384]{2,1,0:T(8,128)(2,1)}, u32[]{:S(2)}, u32[]{:S(2)}) collective-permute-start(bf16[128,32,384]{2,1,0:T(8,128)(2,1)} %project.10.refs_0_.refs_18_), channel_id=1, source_target_pairs={{0,1},{1,0},{2,3},{3,2},{4,5},{5,4},{6,7},{7,6},{8,9},{9,8},{10,11... | collective-permute-start | bytes 9437192 | tf_op jit(solution)/shard_map/ppermute | solution.py:305
  125.2 10.5 %collective-permute-start.6 = (bf16[128,32,384]{2,1,0:T(8,128)(2,1)}, bf16[128,32,384]{2,1,0:T(8,128)(2,1)}, u32[]{:S(2)}, u32[]{:S(2)}) collective-permute-start(bf16[128,32,384]{2,1,0:T(8,128)(2,1)} %get-tuple-element.27.refs_5_.refs_2_), channel_id=1, source_target_pairs={{0,1},{1,0},{2,3},{3,2},{4,5},{5,4},{6,7},{7,6},{8,9},{9,8},{10,11... | collective-permute-start | bytes 9437192 | tf_op jit(solution)/shard_map/ppermute | solution.py:305
  128.4 37.4 %collective-permute-start.10 = (bf16[16,384,128]{2,1,0:T(8,128)(2,1)}, bf16[16,384,128]{2,1,0:T(8,128)(2,1)}, u32[]{:S(2)}, u32[]{:S(2)}) collective-permute-start(bf16[16,384,128]{2,1,0:T(8,128)(2,1)} %slice.7), channel_id=1, source_target_pairs={{0,2},{1,7},{2,4},{3,1},{4,6},{5,3},{6,0},{7,5},{8,10},{9,15},{10,... | collective-permute-start | bytes 4718600 | tf_op jit(solution)/shard_map/ppermute | solution.py:305
  131.9 42.8 %collective-permute-start.9 = (bf16[16,384,128]{2,1,0:T(8,128)(2,1)}, bf16[16,384,128]{2,1,0:T(8,128)(2,1)}, u32[]{:S(2)}, u32[]{:S(2)}) collective-permute-start(bf16[16,384,128]{2,1,0:T(8,128)(2,1)} %slice.7), channel_id=1, source_target_pairs={{0,6},{1,3},{2,0},{3,5},{4,2},{5,7},{6,4},{7,1},{8,14},{9,11},{10,... | collective-permute-start | bytes 4718600 | tf_op jit(solution)/shard_map/ppermute | solution.py:305
  174.7 9.8 %collective-permute-start.11 = (bf16[128,16,384]{2,1,0:T(8,128)(2,1)}, bf16[128,16,384]{2,1,0:T(8,128)(2,1)}, u32[]{:S(2)}, u32[]{:S(2)}) collective-permute-start(bf16[128,16,384]{2,1,0:T(8,128)(2,1)} %get-tuple-element.31.refs_5_.refs_2_), channel_id=1, source_target_pairs={{0,1},{1,0},{2,3},{3,2},{4,5},{5,4},{6,7},{7,6},{8,9},{9,8},{10,11... | collective-permute-start | bytes 4718600 | tf_op jit(solution)/shard_map/ppermute | solution.py:305
  180.6 25.7 %collective-permute-start.12 = (bf16[128,16,384]{2,1,0:T(8,128)(2,1)}, bf16[128,16,384]{2,1,0:T(8,128)(2,1)}, u32[]{:S(2)}, u32[]{:S(2)}) collective-permute-start(bf16[128,16,384]{2,1,0:T(8,128)(2,1)} %project.12.refs_2_.refs_18_.refs_0_), channel_id=1, source_target_pairs={{0,1},{1,0},{2,3},{3,2},{4,5},{5,4},{6,7},{7,6},{8,9},{9,8},{10,11... | collective-permute-start | bytes 4718600 | tf_op jit(solution)/shard_map/ppermute | solution.py:305
  181.1 40.5 %collective-permute-start.1 = (bf16[48,96,128]{2,1,0:T(8,128)(2,1)}, bf16[48,96,128]{2,1,0:T(8,128)(2,1)}, u32[]{:S(2)}, u32[]{:S(2)}) collective-permute-start(bf16[48,96,128]{2,1,0:T(8,128)(2,1)} %triangle.6.refs_5_.refs_0_), channel_id=1, source_target_pairs={{0,2},{1,7},{2,4},{3,1},{4,6},{5,3},{6,0},{7,5},{8,10},{9,15},{10,... | collective-permute-start | bytes 3538952 | tf_op jit(solution)/shard_map/ppermute | solution.py:305
  201.6 28.8 %collective-permute-start.14 = (bf16[48,96,128]{2,1,0:T(8,128)(2,1)}, bf16[48,96,128]{2,1,0:T(8,128)(2,1)}, u32[]{:S(2)}, u32[]{:S(2)}) collective-permute-start(bf16[48,96,128]{2,1,0:T(8,128)(2,1)} %triangle.8.refs_18_.refs_3_), channel_id=1, source_target_pairs={{0,6},{1,3},{2,0},{3,5},{4,2},{5,7},{6,4},{7,1},{8,14},{9,11},{10,... | collective-permute-start | bytes 3538952 | tf_op jit(solution)/shard_map/ppermute | solution.py:305
  201.8 48.4 %collective-permute-start.8 = (bf16[48,128,128]{2,1,0:T(8,128)(2,1)}, bf16[48,128,128]{2,1,0:T(8,128)(2,1)}, u32[]{:S(2)}, u32[]{:S(2)}) collective-permute-start(bf16[48,128,128]{2,1,0:T(8,128)(2,1)} %triangle.7.refs_8_.refs_1_), channel_id=1, source_target_pairs={{0,2},{1,7},{2,4},{3,1},{4,6},{5,3},{6,0},{7,5},{8,10},{9,15},{10,... | collective-permute-start | bytes 4718600 | tf_op jit(solution)/shard_map/ppermute | solution.py:305
  206.3 71.0 %collective-permute-start.15 = (bf16[48,96,128]{2,1,0:T(8,128)(2,1)}, bf16[48,96,128]{2,1,0:T(8,128)(2,1)}, u32[]{:S(2)}, u32[]{:S(2)}) collective-permute-start(bf16[48,96,128]{2,1,0:T(8,128)(2,1)} %triangle.6.refs_5_.refs_0_), channel_id=1, source_target_pairs={{0,6},{1,3},{2,0},{3,5},{4,2},{5,7},{6,4},{7,1},{8,14},{9,11},{10,... | collective-permute-start | bytes 3538952 | tf_op jit(solution)/shard_map/ppermute | solution.py:305
  206.3 71.0 %collective-permute-start.16 = (bf16[48,128,128]{2,1,0:T(8,128)(2,1)}, bf16[48,128,128]{2,1,0:T(8,128)(2,1)}, u32[]{:S(2)}, u32[]{:S(2)}) collective-permute-start(bf16[48,128,128]{2,1,0:T(8,128)(2,1)} %triangle.7.refs_8_.refs_1_), channel_id=1, source_target_pairs={{0,6},{1,3},{2,0},{3,5},{4,2},{5,7},{6,4},{7,1},{8,14},{9,11},{10,... | collective-permute-start | bytes 4718600 | tf_op jit(solution)/shard_map/ppermute | solution.py:305
  221.6 34.2 %collective-permute-start.13 = (bf16[48,64,128]{2,1,0:T(8,128)(2,1)}, bf16[48,64,128]{2,1,0:T(8,128)(2,1)}, u32[]{:S(2)}, u32[]{:S(2)}) collective-permute-start(bf16[48,64,128]{2,1,0:T(8,128)(2,1)} %triangle.9.refs_2_.refs_8_), channel_id=1, source_target_pairs={{0,2},{1,7},{2,4},{3,1},{4,6},{5,3},{6,0},{7,5},{8,10},{9,15},{10,... | collective-permute-start | bytes 2359304 | tf_op jit(solution)/shard_map/ppermute | solution.py:305
  230.5 63.7 %collective-permute-start.18 = (bf16[48,96,128]{2,1,0:T(8,128)(2,1)}, bf16[48,96,128]{2,1,0:T(8,128)(2,1)}, u32[]{:S(2)}, u32[]{:S(2)}) collective-permute-start(bf16[48,96,128]{2,1,0:T(8,128)(2,1)} %collective-permute-done.14.refs_3_), channel_id=1, source_target_pairs={{0,6},{1,3},{2,0},{3,5},{4,2},{5,7},{6,4},{7,1},{8,14},{9,11},{10,... | collective-permute-start | bytes 3538952 | tf_op jit(solution)/shard_map/ppermute | solution.py:305
  250.2 44.0 %collective-permute-start.17 = (bf16[48,64,128]{2,1,0:T(8,128)(2,1)}, bf16[48,64,128]{2,1,0:T(8,128)(2,1)}, u32[]{:S(2)}, u32[]{:S(2)}) collective-permute-start(bf16[48,64,128]{2,1,0:T(8,128)(2,1)} %triangle.9.refs_2_.refs_8_), channel_id=1, source_target_pairs={{0,6},{1,3},{2,0},{3,5},{4,2},{5,7},{6,4},{7,1},{8,14},{9,11},{10,... | collective-permute-start | bytes 2359304 | tf_op jit(solution)/shard_map/ppermute | solution.py:305
  274.8 33.7 %collective-permute-start.19 = (bf16[128,48,384]{2,1,0:T(8,128)(2,1)}, bf16[128,48,384]{2,1,0:T(8,128)(2,1)}, u32[]{:S(2)}, u32[]{:S(2)}) collective-permute-start(bf16[128,48,384]{2,1,0:T(8,128)(2,1)} %get-tuple-element.37.refs_8_.refs_4_), channel_id=1, source_target_pairs={{0,1},{1,0},{2,3},{3,2},{4,5},{5,4},{6,7},{7,6},{8,9},{9,8},{10,11... | collective-permute-start | bytes 14155784 | tf_op jit(solution)/shard_map/ppermute | solution.py:305
  277.3 47.2 %collective-permute-start.21 = (bf16[128,48,384]{2,1,0:T(8,128)(2,1)}, bf16[128,48,384]{2,1,0:T(8,128)(2,1)}, u32[]{:S(2)}, u32[]{:S(2)}) collective-permute-start(bf16[128,48,384]{2,1,0:T(8,128)(2,1)} %get-tuple-element.35.refs_8_.refs_0_), channel_id=1, source_target_pairs={{0,1},{1,0},{2,3},{3,2},{4,5},{5,4},{6,7},{7,6},{8,9},{9,8},{10,11... | collective-permute-start | bytes 14155784 | tf_op jit(solution)/shard_map/ppermute | solution.py:305
  307.9 16.6 %collective-permute-start.22 = (bf16[128,48,384]{2,1,0:T(8,128)(2,1)}, bf16[128,48,384]{2,1,0:T(8,128)(2,1)}, u32[]{:S(2)}, u32[]{:S(2)}) collective-permute-start(bf16[128,48,384]{2,1,0:T(8,128)(2,1)} %project.15.refs_0_.refs_12_.refs_2_), channel_id=1, source_target_pairs={{0,1},{1,0},{2,3},{3,2},{4,5},{5,4},{6,7},{7,6},{8,9},{9,8},{10,11... | collective-permute-start | bytes 14155784 | tf_op jit(solution)/shard_map/ppermute | solution.py:305
  323.1 31.9 %collective-permute-start.20 = (bf16[48,96,128]{2,1,0:T(8,128)(2,1)}, bf16[48,96,128]{2,1,0:T(8,128)(2,1)}, u32[]{:S(2)}, u32[]{:S(2)}) collective-permute-start(bf16[48,96,128]{2,1,0:T(8,128)(2,1)} %triangle.10.refs_24_), channel_id=1, source_target_pairs={{0,6},{1,3},{2,0},{3,5},{4,2},{5,7},{6,4},{7,1},{8,14},{9,11},{10,... | collective-permute-start | bytes 3538952 | tf_op jit(solution)/shard_map/ppermute | solution.py:305
